TPU v7x, 32 devices: a whole 2x2x4 slice. The times are simulated.
32 devices in a mesh: dp: 8 (over z, y), seq: 4 (over x, core).
Axes of the slice: x: 2, y: 2, z: 4, core: 2. Of those that a mesh axis runs over, the one named last changes fastest.
Arguments:
- layer_input: bfloat16 [8, 512, 2048], P('dp', 'seq'), may hold values from -6 to 6
- writes_first: bfloat16 [8, 512, 128], P('dp', 'seq'), may hold values from -0.375 to 0.375
- reads_first: bfloat16 [8, 512, 128], P('dp', 'seq'), may hold values from -0.375 to 0.375
- decay_first: float32 [8, 32, 512], P('dp', None, 'seq'), may hold values from -1.5 to 0, as said below
- skip_first: float32 [32], replicated, may hold values from 0.5 to 1.5
- writes_second: bfloat16 [8, 512, 128], P('dp', 'seq'), may hold values from -0.375 to 0.375
- reads_second: bfloat16 [8, 512, 128], P('dp', 'seq'), may hold values from -0.375 to 0.375
- decay_second: float32 [8, 32, 512], P('dp', None, 'seq'), may hold values from -1.5 to 0, as said below
- skip_second: float32 [32], replicated, may hold values from 0.5 to 1.5
- order_first: int32 [512], P('seq'), may hold values from 0 to 511, as said below
- order_second: int32 [512], P('seq'), may hold values from 0 to 511, as said below
- cotangent: float32 [8, 512, 2048], P('dp', 'seq'), may hold values from -48 to 48
Outputs:
- grad_input: bfloat16 [8, 512, 2048], P('dp', 'seq')
- grad_writes_first: bfloat16 [8, 512, 128], P('dp', 'seq')
- grad_reads_first: bfloat16 [8, 512, 128], P('dp', 'seq')
- grad_decay_first: float32 [8, 32, 512], P('dp', None, 'seq')
- grad_skip_first: float32 [32], replicated
- grad_writes_second: bfloat16 [8, 512, 128], P('dp', 'seq')
- grad_reads_second: bfloat16 [8, 512, 128], P('dp', 'seq')
- grad_decay_second: float32 [8, 32, 512], P('dp', None, 'seq')
- grad_skip_second: float32 [32], replicated
Inputs may be any that keep to these rules, and one draw needn't show every extreme that they name: order_first lists the cells of a 16 by 32 grid (cell i * 32 + j for row i, column j) row after row from row 0 on, each row left to right or right to left. order_second lists the same cells column after column from column 0 on, each column top to bottom or bottom to top. `decay_first`: every entry is negative. `decay_second`: every entry is negative.
All inputs are finite; a program needn't handle non-finite values.
Results may differ from a plain program's by a relative error of at most 0.005.
Values may be sent and summed in bfloat16 or wider, within the bound.
A program may use at most 128 MiB of HBM per device.

v0:
```python
import functools
import math

import jax
import jax.numpy as jnp
from jax import lax
from jax.experimental import pallas as pl
from jax.experimental.pallas import tpu as pltpu
from jax.sharding import PartitionSpec as P

MESH = pl.DeviceIdType.MESH
HIGHEST = lax.Precision.HIGHEST
F32 = jnp.float32
BF16 = jnp.bfloat16


def nn(a, b, precision=None):
    return lax.dot_general(a, b, (((1,), (0,)), ((), ())), precision=precision, preferred_element_type=F32)


def nt(a, b, precision=None):
    return lax.dot_general(a, b, (((1,), (1,)), ((), ())), precision=precision, preferred_element_type=F32)


def tn(a, b, precision=None):
    return lax.dot_general(a, b, (((0,), (0,)), ((), ())), precision=precision, preferred_element_type=F32)


def iota(shape, dim):
    return lax.broadcasted_iota(jnp.int32, shape, dim)


def two(a):
    high = a.astype(BF16)
    return high, (a - high.astype(F32)).astype(BF16)


def nn2(a, b):
    high, low = two(a)
    return nn(high, b) + nn(low, b)


def nt2(a, b):
    high, low = two(b)
    return nt(a, high) + nt(a, low)


def tn2(a, b):
    high, low = two(a)
    return tn(high, b) + tn(low, b)


def spread(x, size):
    per = 128 // size
    rows, heads = x.shape
    lane = iota((rows, 128), 1) // size
    parts = []
    for j in range(heads // per):
        part = jnp.broadcast_to(x[:, per * j : per * j + 1], (rows, 128))
        for k in range(1, per):
            part = jnp.where(lane == k, x[:, per * j + k : per * j + k + 1], part)
        parts.append(part)
    return jnp.concatenate(parts, axis=1)


def split_heads(x, size):
    lane = iota(x.shape, 1) // size
    return jnp.concatenate([jnp.where(lane == k, x, jnp.zeros_like(x)) for k in range(128 // size)], axis=0)


def scale_rows(state, factor, size):
    heads = factor.shape[0]
    return jnp.concatenate(
        [state[h * size : (h + 1) * size] * factor[h : h + 1] for h in range(heads)], axis=0
    )


class Chunk:
    def __init__(self, log_decay, size):
        heads, length = log_decay.shape
        self.size, self.heads, self.length = size, heads, length
        before = (iota((length, length), 0) <= iota((length, length), 1)).astype(F32)
        after = (iota((length, length), 1) <= iota((length, length), 0)).astype(F32)
        self.row = nn(log_decay, before, HIGHEST)
        self.col = nt(after, log_decay, HIGHEST)
        total = self.col[length - 1 : length, :]
        self.grown = jnp.exp(self.col)
        self.left = jnp.exp(total - self.col)
        self.total = jnp.exp(self.row[:, length - 1 : length])

    def gaps(self, h):
        gap = self.col[:, h : h + 1] - self.row[h : h + 1, :]
        causal = iota(gap.shape, 0) >= iota(gap.shape, 1)
        return jnp.where(causal, jnp.exp(jnp.minimum(gap, 0.0)), 0.0)

    def gaps_turned(self, h):
        gap = self.row[h : h + 1, :] - self.col[:, h : h + 1]
        causal = iota(gap.shape, 0) <= iota(gap.shape, 1)
        return jnp.where(causal, jnp.exp(jnp.minimum(gap, 0.0)), 0.0)


def layer_forward(u, w, r, chunk, skip, state):
    size = chunk.size
    per = 128 // size
    scores = nt(r, w)
    outputs = []
    for j in range(chunk.heads // per):
        weights = jnp.concatenate(
            [chunk.gaps(per * j + k) * scores for k in range(per)], axis=1
        )
        outputs.append(nn2(weights, split_heads(u[:, 128 * j : 128 * (j + 1)], size)))
    wide = u.astype(F32)
    y = jnp.concatenate(outputs, axis=1) + spread(chunk.grown, size) * nt2(r, state) + skip * wide
    scaled = wide * spread(chunk.left, size)
    return y, scale_rows(state, chunk.total, size) + tn2(scaled, w)


def layer_back(dy, w, r, chunk, skip, adjoint):
    size = chunk.size
    per = 128 // size
    scores = nt(w, r)
    outputs = []
    for j in range(chunk.heads // per):
        weights = jnp.concatenate(
            [chunk.gaps_turned(per * j + k) * scores for k in range(per)], axis=1
        )
        outputs.append(nn2(weights, split_heads(dy[:, 128 * j : 128 * (j + 1)], size)))
    wide = dy.astype(F32)
    du = jnp.concatenate(outputs, axis=1) + spread(chunk.left, size) * nt2(w, adjoint) + skip * wide
    scaled = wide * spread(chunk.grown, size)
    return du, scale_rows(adjoint, chunk.total, size) + tn2(scaled, r)


def layer_grads(u, dy, w, r, chunk, skip, state, adjoint, want_input):
    size, heads, length = chunk.size, chunk.heads, chunk.length
    per = 128 // size
    features = heads * size
    scores = nt(w, r)
    since = (iota((length, length), 0) >= iota((length, length), 1)).astype(BF16)
    earlier = iota((length, length), 0) < iota((length, length), 1)
    picks = (iota((heads, features), 1) // size == iota((heads, features), 0)).astype(BF16)
    dscores = jnp.zeros((length, length), F32)
    rows, outputs = [], []
    for j in range(heads // per):
        lanes = slice(128 * j, 128 * (j + 1))
        crossed = nt(split_heads(u[:, lanes], size), dy[:, lanes])
        moved, weights = [], []
        for k in range(per):
            gap = chunk.gaps_turned(per * j + k)
            part = gap * crossed[k * length : (k + 1) * length]
            dscores = dscores + part
            moved.append((part * scores).astype(BF16))
            if want_input:
                weights.append((gap * scores).astype(BF16))
        sums = nn(jnp.concatenate(moved, axis=0), since)
        for k in range(per):
            rows.append(
                jnp.sum(
                    jnp.where(earlier, sums[k * length : (k + 1) * length], 0.0), axis=0, keepdims=True
                )
            )
        if want_input:
            outputs.append(nn(jnp.concatenate(weights, axis=1), split_heads(dy[:, lanes], size)))
    wide_u, wide_dy = u.astype(F32), dy.astype(F32)
    left = spread(chunk.left, size)
    dy_scaled = wide_dy * spread(chunk.grown, size)
    u_scaled = wide_u * left
    dy_low, u_low = dy_scaled.astype(BF16), u_scaled.astype(BF16)
    state_low, adjoint_low = state.astype(BF16), adjoint.astype(BF16)
    dscores = dscores.astype(BF16)
    dreads = tn(dscores, w) + nn(dy_low, state_low)
    dwrites = nn(dscores, r) + nn(u_low, adjoint_low)
    read = nt(r, state_low)
    back = nt(w, adjoint_low)
    come = nt(picks, (dy_scaled * read).astype(BF16))
    gone = nt(picks, (u_scaled * back).astype(BF16))
    through = jnp.sum(nn(picks, (state * adjoint).astype(BF16)), axis=1, keepdims=True) * chunk.total
    ddecay = (
        jnp.concatenate(rows, axis=0)
        + nn(come.astype(BF16), since)
        + nn(gone.astype(BF16), earlier.astype(BF16))
        + through
    )
    if want_input:
        du = jnp.concatenate(outputs, axis=1) + left * back + skip * wide_dy
        return dwrites, dreads, ddecay, du, scale_rows(adjoint, chunk.total, size) + tn(dy_low, r)
    return dwrites, dreads, ddecay, None, scale_rows(state, chunk.total, size) + tn(u_low, w)


def whole_kernel(n, clips, size, *refs):
    (u, w1, r1, g1, k1, w2, r2, g2, k2, o1, o2, ct) = refs[:12]
    (dinput, params1_in, params2_in, decays1_in, decays2_in, parts_in) = refs[12:18]
    (u1, w1_all, r1_all, g1_all, w2_all, r2_all, g2_all, o1_all, o2_all, ct_high, ct_low) = refs[18:29]
    (high_out, low_out, y1, du2_high, du2, u2, dy1, states, adjoints, state, adjoint) = refs[29:40]
    (du1, params1, params2, decays1, decays2, skips, clips_in, summed) = refs[40:48]
    (send, recv, out_send, out_recv, clip_send, clip_recv, near_send, near_recv) = refs[48:]
    me, clip = lax.axis_index("seq"), lax.axis_index("dp")
    heads, length = g1.shape[1:]
    features = heads * size
    here = pl.ds(pl.multiple_of(me * features, features), features)

    barrier = pltpu.get_barrier_semaphore()
    for d in range(1, n):
        pl.semaphore_signal(barrier, inc=1, device_id={"seq": lax.rem(me + d, n)}, device_id_type=MESH)
    for d in range(1, clips):
        pl.semaphore_signal(barrier, inc=1, device_id={"dp": lax.rem(clip + d, clips)}, device_id_type=MESH)
    high, low = two(ct[...])
    high_out[...] = high
    low_out[...] = low
    pl.semaphore_wait(barrier, n + clips - 2)

    def copy_to(axis, to, src, dst, one, other):
        return pltpu.make_async_remote_copy(
            src_ref=src, dst_ref=dst, send_sem=one, recv_sem=other, device_id={axis: to}, device_id_type=MESH
        )

    def cut(ref, at):
        return ref.at[:, pl.ds(pl.multiple_of(at * features, features), features)]

    moves = [
        lambda to: (g2.at[to], g2_all.at[me]),
        lambda to: (cut(high_out, to), ct_high.at[me]),
        lambda to: (g1.at[to], g1_all.at[me]),
        lambda to: (cut(u, to), u1.at[me]),
        lambda to: (o1, o1_all.at[me]),
        lambda to: (o2, o2_all.at[me]),
        lambda to: (cut(low_out, to), ct_low.at[me]),
    ]
    twin = me + 1 - 2 * lax.rem(me, 2)
    pairs = ((w2, w2_all), (r2, r2_all), (w1, w1_all), (r1, r1_all))
    far, near = [], []
    for k, (src, dst) in enumerate(pairs):
        for d in range(2, n, 2):
            at = d // 2 - 1
            copy = copy_to("seq", lax.rem(me + d, n), src, dst.at[me], near_send.at[at, k], near_recv.at[at, k])
            copy.start()
            far.append(copy)
        at = n // 2 - 1
        copy = copy_to("seq", twin, src, dst.at[me], near_send.at[at, k], near_recv.at[at, k])
        copy.start()
        near.append(copy)
    arriving = []
    for k, move in enumerate(moves):
        arriving.append([])
        for d in range(1, n):
            to = lax.rem(me + d, n)
            src, dst = move(to)
            copy = copy_to("seq", to, src, dst, send.at[d - 1, k], recv.at[d - 1, k])
            copy.start()
            arriving[k].append(copy)
    for src, dst in ((g1, g1_all), (g2, g2_all)):
        dst[me] = src[me]
    for src, dst in pairs + ((o1, o1_all), (o2, o2_all)):
        dst[me] = src[...]
    u1[me] = u[:, here]
    ct_high[me] = high_out[:, here]
    ct_low[me] = low_out[:, here]

    first = me * heads

    def gains(ref):
        channel = iota((1, features), 1) // size
        row = jnp.zeros((1, features), F32)
        for h in range(heads):
            row = jnp.where(channel == h, ref[first + h], row)
        return row

    skip1, skip2 = gains(k1), gains(k2)
    state[...] = jnp.zeros_like(state)
    adjoint[...] = jnp.zeros_like(adjoint)

    for copy in far:
        copy.wait_recv()
    for k, (src, dst) in enumerate(pairs):
        for d in range(2, n, 2):
            at, block = n // 2 + d // 2 - 1, lax.rem(me - d + n, n)
            copy = copy_to("seq", twin, dst.at[block], dst.at[block], near_send.at[at, k], near_recv.at[at, k])
            copy.start()
            near.append(copy)
    for copy in near:
        copy.wait_recv()
    for k in range(0, 2):
        for copy in arriving[k]:
            copy.wait_recv()

    def back_second(i, carry):
        b = n - 1 - i
        adjoints[b] = adjoint[...]
        du, new = layer_back(ct_high[b], w2_all[b], r2_all[b], Chunk(g2_all[b], size), skip2, adjoint[...])
        du2_high[b] = du
        adjoint[...] = new
        return carry

    lax.fori_loop(0, n, back_second, 0, unroll=2)
    for k in range(2, 4):
        for copy in arriving[k]:
            copy.wait_recv()

    def forward_first(i, carry):
        states[i] = state[...]
        y, new = layer_forward(u1[i], w1_all[i], r1_all[i], Chunk(g1_all[i], size), skip1, state[...])
        y1[i] = y.astype(BF16)
        state[...] = new
        return carry

    lax.fori_loop(0, n, forward_first, 0, unroll=2)
    for k in range(4, 6):
        for copy in arriving[k]:
            copy.wait_recv()

    def cells(ref, i):
        return jnp.transpose(jnp.broadcast_to(ref[i].astype(F32), (length, length)))

    def regrid(i, carry):
        second = cells(o2_all, i)
        total = jnp.zeros((length, features), F32)
        for j in range(n):
            take = (second == o1_all[j].astype(F32)).astype(BF16)
            total = total + nn(take, y1[j])
        u2[i] = total.astype(BF16)
        return carry

    lax.fori_loop(0, n, regrid, 0)

    state[...] = jnp.zeros_like(state)
    adjoint[...] = jnp.zeros_like(adjoint)

    def leave_second(to, slot):
        return [
            copy_to("seq", to, params2.at[to], params2_in.at[me], out_send.at[slot, 0], out_recv.at[slot, 0]),
            copy_to("seq", to, decays2.at[to], decays2_in.at[me], out_send.at[slot, 1], out_recv.at[slot, 1]),
        ]

    def leave_first(to, slot):
        return [
            copy_to("seq", to, du1.at[to], dinput.at[:, here], out_send.at[slot, 2], out_recv.at[slot, 2]),
            copy_to("seq", to, params1.at[to], params1_in.at[me], out_send.at[slot, 3], out_recv.at[slot, 3]),
            copy_to("seq", to, decays1.at[to], decays1_in.at[me], out_send.at[slot, 4], out_recv.at[slot, 4]),
        ]

    def grads_second(i, carry):
        dw, dr, dg, _, new = layer_grads(
            u2[i], ct_high[i], w2_all[i], r2_all[i], Chunk(g2_all[i], size), skip2, state[...], adjoints[i], False
        )
        state[...] = new
        params2[i, 0] = dw.astype(BF16)
        params2[i, 1] = dr.astype(BF16)
        decays2[i] = dg

        @pl.when(i != me)
        def _():
            for copy in leave_second(i, lax.rem(i - me + n, n) - 1):
                copy.start()

        return carry

    lax.fori_loop(0, n, grads_second, 0)
    for copy in arriving[6]:
        copy.wait_recv()
    skips[...] = jnp.zeros_like(skips)

    def finish_back(i, carry):
        rest = ct_low[i].astype(F32)
        du2[i] = (du2_high[i] + skip2 * rest).astype(BF16)
        upstream = ct_high[i].astype(F32) + rest
        skips[1:2, :] += jnp.sum(upstream * u2[i].astype(F32), axis=0, keepdims=True)
        return carry

    lax.fori_loop(0, n, finish_back, 0)

    def regrid_back(i, carry):
        cell = cells(o1_all, i)
        total = jnp.zeros((length, features), F32)
        for j in range(n):
            take = (cell == o2_all[j].astype(F32)).astype(BF16)
            total = total + nn(take, du2[j])
        dy1[i] = total.astype(BF16)
        skips[0:1, :] += jnp.sum(u1[i].astype(F32) * total, axis=0, keepdims=True)
        return carry

    lax.fori_loop(0, n, regrid_back, 0)
    clip_copies = []
    for d in range(1, clips):
        to = lax.rem(clip + d, clips)
        copy = copy_to("dp", to, skips, clips_in.at[clip], clip_send.at[d - 1], clip_recv.at[d - 1])
        copy.start()
        clip_copies.append(copy)
    clips_in[clip] = skips[...]

    def grads_first(i, carry):
        b = n - 1 - i
        dw, dr, dg, du, new = layer_grads(
            u1[b], dy1[b], w1_all[b], r1_all[b], Chunk(g1_all[b], size), skip1, states[b], adjoint[...], True
        )
        adjoint[...] = new
        du1[b] = du.astype(BF16)
        params1[b, 0] = dw.astype(BF16)
        params1[b, 1] = dr.astype(BF16)
        decays1[b] = dg

        @pl.when(b != me)
        def _():
            for copy in leave_first(b, lax.rem(b - me + n, n) - 1):
                copy.start()

        return carry

    lax.fori_loop(0, n, grads_first, 0)
    for copy in clip_copies:
        copy.wait()
    summed[...] = jnp.sum(clips_in[...], axis=0)
    last = []
    for d in range(1, n):
        to = lax.rem(me + d, n)
        copy = copy_to("seq", to, summed, parts_in.at[me], out_send.at[d - 1, 5], out_recv.at[d - 1, 5])
        copy.start()
        last.append(copy)
    parts_in[me] = summed[...]
    params1_in[me] = params1[me]
    params2_in[me] = params2[me]
    decays1_in[me] = decays1[me]
    decays2_in[me] = decays2[me]
    dinput[:, here] = du1[me]
    for group in arriving:
        for copy in group:
            copy.wait_send()
    for copy in far + near:
        copy.wait_send()
    for d in range(1, n):
        to = lax.rem(me + d, n)
        last += leave_second(to, d - 1) + leave_first(to, d - 1)
    for copy in last:
        copy.wait()


def whole(n, clips, size, u, w1, r1, g1, k1, w2, r2, g2, k2, o1, o2, ct):
    length, width = u.shape
    heads = g1.shape[1]
    count = w1.shape[1]
    features = heads * size
    vmem = pl.BlockSpec(memory_space=pltpu.VMEM)
    smem = pl.BlockSpec(memory_space=pltpu.SMEM)
    wide, param, params = (n, length, features), (n, length, count), (n, 2, length, count)
    decay, order, gain = (n, heads, length), (n, 1, length), (2, features)
    outs = (((length, width), BF16), (params, BF16), (params, BF16), (decay, F32), (decay, F32), ((n,) + gain, F32))
    held = [
        (wide, BF16),
        (param, BF16),
        (param, BF16),
        (decay, F32),
        (param, BF16),
        (param, BF16),
        (decay, F32),
        (order, jnp.int32),
        (order, jnp.int32),
        (wide, BF16),
        (wide, BF16),
        ((length, width), BF16),
        ((length, width), BF16),
        (wide, BF16),
        (wide, F32),
        (wide, BF16),
        (wide, BF16),
        (wide, BF16),
        ((n, features, count), F32),
        ((n, features, count), F32),
        ((features, count), F32),
        ((features, count), F32),
        (wide, BF16),
        (params, BF16),
        (params, BF16),
        (decay, F32),
        (decay, F32),
        (gain, F32),
        ((clips,) + gain, F32),
        (gain, F32),
    ]
    return pl.pallas_call(
        functools.partial(whole_kernel, n, clips, size),
        out_shape=tuple(jax.ShapeDtypeStruct(*out) for out in outs),
        in_specs=[vmem] * 4 + [smem] + [vmem] * 3 + [smem] + [vmem] * 3,
        out_specs=[vmem] * 6,
        scratch_shapes=[pltpu.VMEM(*one) for one in held]
        + [pltpu.SemaphoreType.DMA((n - 1, 7))] * 2
        + [pltpu.SemaphoreType.DMA((n - 1, 6))] * 2
        + [pltpu.SemaphoreType.DMA((clips - 1,))] * 2
        + [pltpu.SemaphoreType.DMA((n - 1, 4))] * 2,
        compiler_params=pltpu.CompilerParams(collective_id=0, has_side_effects=True),
        name="whole",
    )(u, w1, r1, g1, k1, w2, r2, g2, k2, o1, o2, ct)


def gather_kernel(n, factor, *refs):
    (du, params1, params2, decays1, decays2, parts) = refs[:6]
    (dinput, dw1, dr1, dg1, dk1, dw2, dr2, dg2, dk2) = refs[6:]
    heads = decays1.shape[1]
    width = parts.shape[2]
    size = width // heads
    dinput[...] = du[...]
    dg1[...] = decays1[...]
    dg2[...] = decays2[...]
    for params, outs in ((params1, (dw1, dr1)), (params2, (dw2, dr2))):
        for k, out in enumerate(outs):
            total = params[0, k].astype(F32)
            for s in range(1, n):
                total = total + params[s, k].astype(F32)
            out[...] = total.astype(BF16)
    picks = (iota((width, heads), 0) // size == iota((width, heads), 1)).astype(F32)
    for s in range(n):
        by_head = nn(parts[s], picks, HIGHEST) * factor
        dk1[:, s * heads : (s + 1) * heads] = by_head[0:1]
        dk2[:, s * heads : (s + 1) * heads] = by_head[1:2]


def gather(n, factor, du, params1, params2, decays1, decays2, parts):
    length, count = params1.shape[2:]
    heads = decays1.shape[1]
    vmem = pl.BlockSpec(memory_space=pltpu.VMEM)
    param = jax.ShapeDtypeStruct((length, count), BF16)
    decay = jax.ShapeDtypeStruct(decays1.shape, F32)
    skip = jax.ShapeDtypeStruct((1, n * heads), F32)
    layer = (param, param, decay, skip)
    return pl.pallas_call(
        functools.partial(gather_kernel, n, factor),
        out_shape=(jax.ShapeDtypeStruct(du.shape, BF16),) + layer + layer,
        in_specs=[vmem] * 6,
        out_specs=[vmem] * 9,
        name="gather",
    )(du, params1, params2, decays1, decays2, parts)


def on_device(n, clips, u, w1, r1, g1, k1, w2, r2, g2, k2, o1, o2, ct):
    length, features = u.shape[1:]
    head_count = k1.shape[0]
    size = features // head_count
    heads = head_count // n

    def by_device(g):
        return g.reshape(n, heads, length)

    results = whole(
        n,
        clips,
        size,
        u[0],
        w1[0],
        r1[0],
        by_device(g1),
        k1,
        w2[0],
        r2[0],
        by_device(g2),
        k2,
        o1[None],
        o2[None],
        ct[0],
    )
    factor = 1.0 / math.sqrt(clips * n * length * size)
    du, dw1, dr1, dg1, dk1, dw2, dr2, dg2, dk2 = gather(n, factor, *results)
    return (
        du[None],
        dw1[None],
        dr1[None],
        dg1.reshape(1, head_count, length),
        dk1[0],
        dw2[None],
        dr2[None],
        dg2.reshape(1, head_count, length),
        dk2[0],
    )


def solution(mesh):
    tokens, decay = P("dp", "seq", None), P("dp", None, "seq")
    return jax.shard_map(
        functools.partial(on_device, mesh.shape["seq"], mesh.shape["dp"]),
        mesh=mesh,
        in_specs=(tokens, tokens, tokens, decay, P(), tokens, tokens, decay, P(), P("seq"), P("seq"), tokens),
        out_specs=(tokens, tokens, tokens, decay, P(), tokens, tokens, decay, P()),
        check_vma=False,
    )
```

profile of v0, /device:TPU:0, one launch (start us, length us, event | category | flops | bytes accessed | tf_op | source)
XLA Modules:
  0.0 55.9 jit_solution(7156159079787352702)
XLA Ops:
  0.6 52.6 %whole.1 = (bf16[128,2048]{1,0:T(8,128)(2,1)}, bf16[4,2,128,128]{3,2,1,0:T(8,128)(2,1)}, bf16[4,2,128,128]{3,2,1,0:T(8,128)(2,1)}, f32[4,8,128]{2,1,0:T(8,128)},...) custom-call(bf16[128,2048]{1,0:T(8,128)(2,1)} %bitcast.20, bf16[128,128]{1,0:T(8,128)(2,1)} %bitcast.21, ...), custom_call_target="tpu_custom_call" | custom-call | tf_op jit(solution)/shard_map/whole/pallas_call | solution.py:478
  53.3 2.6 %gather.1 = (bf16[128,2048]{1,0:T(8,128)(2,1)}, bf16[128,128]{1,0:T(8,128)(2,1)}, bf16[128,128]{1,0:T(8,128)(2,1)}, f32[4,8,128]{2,1,0:T(8,128)}, f32[1,32]{1,0:...) custom-call(bf16[128,2048]{1,0:T(8,128)(2,1)} %get-tuple-element.24.refs, ...), custom_call_target="tpu_custom_call" | custom-call | tf_op jit(solution)/shard_map/gather/pallas_call | solution.py:523
where the time goes:
time: 56.1 us; the launch traced here: 55.9 us
  Pallas kernels  55.3 us (99%)
  between operations  0.65 us (1%)
    pallas_call x1, Pallas kernels, whole(): pl.pallas_call(functools.partial(whole_kernel, n, clips, size), out_shape...  52.6 us
    pallas_call x1, Pallas kernels, gather(): pl.pallas_call(functools.partial(gather_kernel, n, factor), out_shape=(ja...  2.62 us

commit v1 on v0

v1 whole, which is shorter than its diff:
```python
import functools
import math
import types

import jax
import jax.numpy as jnp
from jax import lax
from jax.experimental import pallas as pl
from jax.experimental.pallas import tpu as pltpu
from jax.sharding import PartitionSpec as P

MESH = pl.DeviceIdType.MESH
HIGHEST = lax.Precision.HIGHEST
F32 = jnp.float32
BF16 = jnp.bfloat16


def nn(a, b, precision=None):
    return lax.dot_general(a, b, (((1,), (0,)), ((), ())), precision=precision, preferred_element_type=F32)


def nt(a, b, precision=None):
    return lax.dot_general(a, b, (((1,), (1,)), ((), ())), precision=precision, preferred_element_type=F32)


def tn(a, b, precision=None):
    return lax.dot_general(a, b, (((0,), (0,)), ((), ())), precision=precision, preferred_element_type=F32)


def iota(shape, dim):
    return lax.broadcasted_iota(jnp.int32, shape, dim)


def two(a):
    high = a.astype(BF16)
    return high, (a - high.astype(F32)).astype(BF16)


def rows_of(*parts):
    return jnp.concatenate(parts, axis=0)


def decay_sums(length):
    half, mid = length // 2, length // 4
    t, s = iota((length + 8, length), 0), iota((length + 8, length), 1)
    first, second = mid, half + mid
    middle = jnp.where(t < half, first, second)
    by_token = (s <= t).astype(F32) - (s < middle).astype(F32)
    k = t - length
    by_chunk = jnp.where(k == 0, (s < first).astype(F32), 0.0)
    by_chunk = jnp.where(k == 1, (s < second).astype(F32), by_chunk)
    by_chunk = jnp.where(k == 2, (s >= first).astype(F32), by_chunk)
    by_chunk = jnp.where(k == 3, (s >= second).astype(F32), by_chunk)
    by_chunk = jnp.where(k == 4, 1.0, by_chunk)
    by_chunk = jnp.where(k == 5, ((s >= first) & (s < second)).astype(F32), by_chunk)
    return jnp.where(k < 0, by_token, by_chunk).astype(BF16)


def factors(log_decay, size):
    heads, length = log_decay.shape
    sums = decay_sums(length)
    wide = [
        jnp.concatenate([jnp.broadcast_to(part[h : h + 1], (size, length)) for h in range(heads)], axis=0).astype(BF16)
        for part in (p.astype(F32) for p in two(log_decay))
    ]
    logs = nt(sums, wide[0]) + nt(sums, wide[1])
    by_token = logs[:length]
    return jnp.exp(by_token), jnp.exp(-by_token), jnp.exp(logs[length:])


def strict_scores(a, b, lower):
    scores = nt(a, b)
    row, col = iota(scores.shape, 0), iota(scores.shape, 1)
    return two(jnp.where(row > col if lower else row < col, scores, 0.0))


def lead(left, scores, low, start, first, second, starts_low=None, parts_low=None):
    both = rows_of(first, second)
    out = nn(jnp.concatenate([left, scores], axis=1), rows_of(start, both))
    if low is not None:
        out = out + nn(low, both)
    if starts_low is not None:
        out = out + nn(jnp.concatenate([left, scores], axis=1), rows_of(starts_low, *parts_low))
    return out


def whole_kernel(n, clips, size, held, sems, *refs):
    x = types.SimpleNamespace(**dict(zip(held, refs[20:])))
    x.u, x.w1, x.r1, x.g1, x.k1, x.w2, x.r2, x.g2, x.k2, x.o1, x.o2, x.ct = refs[:12]
    x.dinput, x.dw1, x.dr1, x.dw2, x.dr2, x.decays1_in, x.decays2_in, x.parts_in = refs[12:20]
    x.__dict__.update(zip(sems, zip(refs[20 + len(held) :: 2], refs[21 + len(held) :: 2])))
    me, clip = lax.axis_index("seq"), lax.axis_index("dp")
    chips = n // 2
    chip, core = lax.div(me, 2), lax.rem(me, 2)
    twin = me + 1 - 2 * core
    heads, length = x.g1.shape[1:]
    features = heads * size
    half = length // 2
    here = pl.ds(pl.multiple_of(me * features, features), features)

    def chunk(b):
        return pl.ds(pl.multiple_of(b * length, length), length)

    barrier = pltpu.get_barrier_semaphore()
    for d in range(1, n):
        pl.semaphore_signal(barrier, inc=1, device_id={"seq": lax.rem(me + d, n)}, device_id_type=MESH)
    for d in range(1, clips):
        pl.semaphore_signal(barrier, inc=1, device_id={"dp": lax.rem(clip + d, clips)}, device_id_type=MESH)
    x.ct_out[...] = x.ct[...].astype(BF16)
    pl.semaphore_wait(barrier, n + clips - 2)

    def copy_to(axis, to, src, dst, pair, *at):
        return pltpu.make_async_remote_copy(
            src_ref=src,
            dst_ref=dst,
            send_sem=pair[0].at[at],
            recv_sem=pair[1].at[at],
            device_id={axis: to},
            device_id_type=MESH,
        )

    def cut(ref, at):
        return ref.at[:, pl.ds(pl.multiple_of(at * features, features), features)]

    def device(away, other):
        return 2 * lax.rem(chip + away, chips) + (1 - core if other else core)

    peers = [(away, other) for away in range(1, chips) for other in (0, 1)] + [(0, 1)]
    moves = [
        lambda to: (x.g2.at[to], x.g_all.at[1, me]),
        lambda to: (cut(x.ct_out, to), x.ct_all.at[me]),
        lambda to: (x.g1.at[to], x.g_all.at[0, me]),
        lambda to: (cut(x.u, to), x.u_all.at[me]),
        lambda to: (x.o1, x.o1_all.at[me]),
        lambda to: (x.o2, x.o2_all.at[me]),
    ]
    arriving = [[] for _ in moves]

    def issue(k):
        for away, other in peers:
            to = device(away, other)
            copy = copy_to("seq", to, *moves[k](to), x.move, 2 * away + other - 1, k)
            copy.start()
            arriving[k].append(copy)

    pairs = ((x.w2, x.w_all.at[1]), (x.r2, x.r_all.at[1]), (x.w1, x.w_all.at[0]), (x.r1, x.r_all.at[0]))
    far, near = [], []

    def issue_pair(k):
        src, dst = pairs[k]
        for away in range(1, chips):
            copy = copy_to("seq", device(away, 0), src, dst.at[me], x.near, away - 1, k)
            copy.start()
            far.append(copy)
        copy = copy_to("seq", twin, src, dst.at[me], x.near, chips - 1, k)
        copy.start()
        near.append(copy)

    def wait_for(k):
        for copy in arriving[k]:
            copy.wait_recv()

    issue_pair(0)
    issue_pair(1)
    issue(0)
    issue(2)
    issue_pair(2)
    issue_pair(3)
    issue(4)
    issue(5)
    issue(1)
    issue(3)
    x.g_all[0, me] = x.g1[me]
    x.g_all[1, me] = x.g2[me]
    for src, dst in pairs + ((x.o1, x.o1_all), (x.o2, x.o2_all)):
        dst[me] = src[...]
    x.u_all[me] = x.u[:, here]
    x.ct_all[me] = x.ct_out[:, here]

    first = me * heads

    def gains(ref):
        channel = iota((1, features), 1) // size
        row = jnp.zeros((1, features), F32)
        for h in range(heads):
            row = jnp.where(channel == h, ref[first + h], row)
        return row

    skips = (gains(x.k1), gains(x.k2))

    def prepare_decays(layer):
        def step(b, carry):
            grown, shrunk, sums = factors(x.g_all[layer, b], size)
            x.grown[layer, b] = grown
            x.shrunk[layer, b] = shrunk
            x.sums[layer, b] = sums
            return carry

        lax.fori_loop(0, n, step, 0)

    def prepare_scores(layer):
        def step(b, carry):
            w, r = x.w_all[layer, b], x.r_all[layer, b]
            x.fore[layer, b], x.fore_low[layer, b] = strict_scores(r, w, True)
            x.back[layer, b], x.back_low[layer, b] = strict_scores(w, r, False)
            return carry

        lax.fori_loop(0, n, step, 0)

    def prepare_order(src, dst, out):
        def step(i, carry):
            cell = jnp.transpose(jnp.broadcast_to(dst[i].astype(F32), (length, length)))
            out[i] = jnp.concatenate([(cell == src[j].astype(F32)).astype(BF16) for j in range(n)], axis=1)
            return carry

        lax.fori_loop(0, n, step, 0)

    wait_for(0)
    prepare_decays(1)
    wait_for(2)
    prepare_decays(0)
    for copy in far:
        copy.wait_recv()
    for k, (src, dst) in enumerate(pairs):
        for away in range(1, chips):
            block = 2 * lax.rem(chip - away + chips, chips) + core
            copy = copy_to("seq", twin, dst.at[block], dst.at[block], x.near, chips - 1 + away, k)
            copy.start()
            near.append(copy)
    wait_for(4)
    wait_for(5)
    prepare_order(x.o2_all, x.o1_all, x.take_first)
    prepare_order(x.o1_all, x.o2_all, x.take_second)
    for copy in near:
        copy.wait_recv()
    prepare_scores(1)
    prepare_scores(0)
    state, adjoint = x.state, x.adjoint
    adjoint[...] = jnp.zeros_like(adjoint)
    state[...] = jnp.zeros_like(state)

    def own(w, r):
        return jnp.sum(w.astype(F32) * r.astype(F32), axis=1, keepdims=True)

    def back(layer, b, dy):
        wide, w, r = dy.astype(F32), x.w_all[layer, b], x.r_all[layer, b]
        sums, scores, low = x.sums[layer, b], x.back[layer, b], x.back_low[layer, b]
        scaled = wide * x.grown[layer, b]
        high = scaled.astype(BF16)
        a, z = high[:half], high[half:]
        turned = (scaled[half:] * sums[5:6]).astype(BF16)
        end = adjoint[...]
        end_a, end_z = (end * sums[2:3]).astype(BF16), (end * sums[3:4]).astype(BF16)
        x.ends[layer, b] = end
        x.ends_a[layer, b] = end_a
        x.ends_z[layer, b] = end_z
        x.dys[layer, b] = high
        top = lead(w[:half], scores[:half], low[:half], end_a, a, turned)
        bottom = lead(w[half:], scores[half:], low[half:], end_z, a, z)
        inner = rows_of(top, bottom) * x.shrunk[layer, b]
        x.inner[layer, b] = inner
        carried = rows_of(scaled[:half] * sums[0:1], scaled[half:] * sums[1:2]).astype(BF16)
        adjoint[...] = end * sums[4:5] + tn(r, carried)
        return inner + (skips[layer] + own(w, r)) * wide

    lower = iota((length, length), 0) >= iota((length, length), 1)
    since = lower.astype(BF16)
    picks = (iota((features, heads), 0) // size == iota((features, heads), 1)).astype(BF16)

    def forward(layer, b, u, dy, precise):
        wide, wide_dy, w, r = u.astype(F32), dy.astype(F32), x.w_all[layer, b], x.r_all[layer, b]
        sums, scores, low = x.sums[layer, b], x.fore[layer, b], x.fore_low[layer, b]
        scaled = wide * x.shrunk[layer, b]
        high, rest = two(scaled)
        a, z, a_low, z_low = high[:half], high[half:], rest[:half], rest[half:]
        turned, turned_low = two(scaled[:half] * sums[5:6])
        start = state[...]
        start_a, start_a_low = two(start * sums[0:1])
        start_z, start_z_low = two(start * sums[1:2])
        if precise:
            top = lead(r[:half], scores[:half], low[:half], start_a, a, z, start_a_low, (a_low, z_low))
            bottom = lead(r[half:], scores[half:], low[half:], start_z, turned, z, start_z_low, (turned_low, z_low))
        else:
            top = lead(r[:half], scores[:half], None, start_a, a, z)
            bottom = lead(r[half:], scores[half:], None, start_z, turned, z)
        inner = rows_of(top, bottom) * x.grown[layer, b]
        carried, carried_low = two(rows_of(scaled[:half] * sums[2:3], scaled[half:] * sums[3:4]))
        after = start * sums[4:5] + tn(w, carried)
        if precise:
            after = after + tn(w, carried_low)
        state[...] = after

        through = jnp.sum(x.ends[layer, b] * after, axis=0, keepdims=True)
        terms = wide_dy * inner - wide * x.inner[layer, b]
        last = terms[length - 8 :] + jnp.where(iota((8, features), 0) == 7, through, 0.0)
        terms, terms_low = two(rows_of(terms[: length - 8], last))
        by_head, by_head_low = two(nn(terms, picks) + nn(terms_low, picks))
        ddecay = tn(by_head, since) + tn(by_head_low, since)

        dys = x.dys[layer, b]
        dy_a, dy_z = dys[:half], dys[half:]
        dscores = rows_of(
            nt(dy_a, high) + nt(dy_a, rest),
            nt(dy_z, rows_of(turned, z)) + nt(dy_z, rows_of(turned_low, z_low)),
        )
        dscores, dscores_low = two(jnp.where(lower, dscores, 0.0))
        dreads = nn(dscores, w) + nn(dscores_low, w) + rows_of(nt(dy_a, start_a), nt(dy_z, start_z))
        dwrites = (
            tn(dscores, r)
            + tn(dscores_low, r)
            + rows_of(nt(a, x.ends_a[layer, b]), nt(z, x.ends_z[layer, b]))
        )
        x.params[layer, b, 0] = dwrites
        x.params[layer, b, 1] = dreads
        x.decays[layer, b] = ddecay
        return inner + (skips[layer] + own(w, r)) * wide

    decays_in = (x.decays1_in, x.decays2_in)

    def input_copy(to, slot):
        return copy_to("seq", to, x.du1.at[to], x.dinput.at[:, here], x.input, slot)

    def decay_copy(layer, to, slot):
        return copy_to("seq", to, x.decays.at[layer, to], decays_in[layer].at[me], x.decay, layer, slot)

    def twin_copy(layer, owner, slot):
        return copy_to("seq", twin, x.params.at[layer, owner], x.twins.at[layer, slot], x.twin, layer, slot)

    def slot_of(to):
        return lax.rem(to - me + n, n) - 1

    def leave(layer, b):
        @pl.when(b != me)
        def _():
            decay_copy(layer, b, slot_of(b)).start()

        @pl.when(lax.rem(b, 2) != core)
        def _():
            twin_copy(layer, b, lax.rem(lax.div(b, 2) - chip + chips, chips)).start()

    chip_copies = []

    def leave_chip(layer):
        for away in range(1, chips):
            owner = device(away, 0)
            twin_copy(layer, device(away, 1), away).wait_recv()
            total = x.params[layer, owner] + x.twins[layer, away]
            x.chip_sums[layer, away] = total.astype(BF16)
            copy = copy_to(
                "seq", owner, x.chip_sums.at[layer, away], x.chips_in.at[layer, away], x.chip, layer, away
            )
            copy.start()
            chip_copies.append(copy)

    wait_for(1)

    def back_second(i, carry):
        b = n - 1 - i
        x.du2[chunk(b)] = back(1, b, x.ct_all[b]).astype(BF16)
        return carry

    lax.fori_loop(0, n, back_second, 0, unroll=2)

    def regrid_back(i, carry):
        x.dy1[chunk(i)] = nn(x.take_first[i], x.du2[...]).astype(BF16)
        return carry

    lax.fori_loop(0, n, regrid_back, 0, unroll=2)
    adjoint[...] = jnp.zeros_like(adjoint)

    def back_first(i, carry):
        b = n - 1 - i
        x.du1[b] = back(0, b, x.dy1[chunk(b)]).astype(BF16)

        @pl.when(b != me)
        def _():
            input_copy(b, slot_of(b)).start()

        return carry

    lax.fori_loop(0, n, back_first, 0)
    wait_for(3)
    x.skips[...] = jnp.zeros_like(x.skips)

    def first_layer(b, carry):
        u, dy = x.u_all[b], x.dy1[chunk(b)]
        x.y1[chunk(b)] = forward(0, b, u, dy, True).astype(BF16)
        x.skips[0:1, :] += jnp.sum(u.astype(F32) * dy.astype(F32), axis=0, keepdims=True)
        leave(0, b)
        return carry

    lax.fori_loop(0, n, first_layer, 0)

    def regrid(i, carry):
        u = nn(x.take_second[i], x.y1[...])
        x.u2[i] = u.astype(BF16)
        x.skips[1:2, :] += jnp.sum(u * x.ct_all[i].astype(F32), axis=0, keepdims=True)
        return carry

    lax.fori_loop(0, n, regrid, 0, unroll=2)
    clip_copies = []
    for d in range(1, clips):
        to = lax.rem(clip + d, clips)
        copy = copy_to("dp", to, x.skips, x.clips_in.at[clip], x.clip, d - 1)
        copy.start()
        clip_copies.append(copy)
    x.clips_in[clip] = x.skips[...]
    leave_chip(0)
    state[...] = jnp.zeros_like(state)

    def second_layer(b, carry):
        forward(1, b, x.u2[b], x.ct_all[b], False)
        leave(1, b)
        return carry

    lax.fori_loop(0, n, second_layer, 0)
    for copy in clip_copies:
        copy.wait()
    x.summed[...] = jnp.sum(x.clips_in[...], axis=0)
    last = []
    for d in range(1, n):
        to = lax.rem(me + d, n)
        copy = copy_to("seq", to, x.summed, x.parts_in.at[me], x.part, d - 1)
        copy.start()
        last.append(copy)
    leave_chip(1)
    x.parts_in[me] = x.summed[...]
    for layer in range(2):
        decays_in[layer][me] = x.decays[layer, me]
    x.dinput[:, here] = x.du1[me]
    for layer, outs in enumerate(((x.dw1, x.dr1), (x.dw2, x.dr2))):
        twin_copy(layer, twin, 0).wait_recv()
        for k, out in enumerate(outs):
            total = x.params[layer, me, k] + x.twins[layer, 0, k]
            if k == 0:
                for copy in chip_copies[layer * (chips - 1) : (layer + 1) * (chips - 1)]:
                    copy.wait_recv()
            for away in range(1, chips):
                total = total + x.chips_in[layer, away, k].astype(F32)
            out[...] = total.astype(BF16)
    for group in arriving:
        for copy in group:
            copy.wait_send()
    for copy in far + near + chip_copies:
        copy.wait_send()
    for layer in range(2):
        for away in range(chips):
            twin_copy(layer, device(away, 1), away).wait_send()
    for d in range(1, n):
        to = lax.rem(me + d, n)
        last += [input_copy(to, d - 1), decay_copy(0, to, d - 1), decay_copy(1, to, d - 1)]
    for copy in last:
        copy.wait()


def whole(n, clips, size, *args):
    length, width = args[0].shape
    heads = args[3].shape[1]
    count = args[1].shape[1]
    features, half, chips = heads * size, length // 2, n // 2
    vmem = pl.BlockSpec(memory_space=pltpu.VMEM)
    smem = pl.BlockSpec(memory_space=pltpu.SMEM)
    param, decay, gain = (length, count), (n, heads, length), (2, features)
    wide, flat, held, square = (n, length, features), (n * length, features), (n, count, features), (n, length, length)
    order, pick, pair = (n, 1, length), (n, length, n * length), (2, length, count)
    outs = (((length, width), BF16),) + ((param, BF16),) * 4 + ((decay, F32),) * 2 + (((n,) + gain, F32),)
    scratch = dict(
        ct_out=((length, width), BF16),
        u_all=(wide, BF16),
        ct_all=(wide, BF16),
        w_all=((2, n) + param, BF16),
        r_all=((2, n) + param, BF16),
        g_all=((2,) + decay, F32),
        o1_all=(order, jnp.int32),
        o2_all=(order, jnp.int32),
        grown=((2,) + wide, F32),
        shrunk=((2,) + wide, F32),
        sums=((2, n, 8, features), F32),
        fore=((2,) + square, BF16),
        fore_low=((2,) + square, BF16),
        back=((2,) + square, BF16),
        back_low=((2,) + square, BF16),
        take_first=(pick, BF16),
        take_second=(pick, BF16),
        du2=(flat, BF16),
        dy1=(flat, BF16),
        y1=(flat, BF16),
        u2=(wide, BF16),
        du1=(wide, BF16),
        dys=((2,) + wide, BF16),
        ends=((2,) + held, F32),
        ends_a=((2,) + held, BF16),
        ends_z=((2,) + held, BF16),
        inner=((2,) + wide, F32),
        state=((count, features), F32),
        adjoint=((count, features), F32),
        params=((2, n) + pair, F32),
        twins=((2, chips) + pair, F32),
        chip_sums=((2, chips) + pair, BF16),
        chips_in=((2, chips) + pair, BF16),
        decays=((2,) + decay, F32),
        skips=(gain, F32),
        clips_in=((clips,) + gain, F32),
        summed=(gain, F32),
    )
    sems = dict(
        move=(n - 1, 6),
        near=(n - 1, 4),
        input=(n - 1,),
        decay=(2, n - 1),
        twin=(2, chips),
        chip=(2, chips),
        clip=(clips - 1,),
        part=(n - 1,),
    )
    return pl.pallas_call(
        functools.partial(whole_kernel, n, clips, size, tuple(scratch), tuple(sems)),
        out_shape=tuple(jax.ShapeDtypeStruct(*out) for out in outs),
        in_specs=[vmem] * 4 + [smem] + [vmem] * 3 + [smem] + [vmem] * 3,
        out_specs=[vmem] * 8,
        scratch_shapes=[pltpu.VMEM(*one) for one in scratch.values()]
        + [pltpu.SemaphoreType.DMA(shape) for shape in sems.values() for _ in range(2)],
        compiler_params=pltpu.CompilerParams(collective_id=0, has_side_effects=True),
        name="whole",
    )(*args)


def gather_kernel(n, factor, *refs):
    parts = refs[7]
    for src, dst in zip(refs[:7], refs[8:15]):
        dst[...] = src[...]
    dk1, dk2 = refs[15:]
    heads = refs[5].shape[1]
    width = parts.shape[2]
    size = width // heads
    picks = (iota((width, heads), 0) // size == iota((width, heads), 1)).astype(F32)
    for s in range(n):
        by_head = nn(parts[s], picks, HIGHEST) * factor
        dk1[:, s * heads : (s + 1) * heads] = by_head[0:1]
        dk2[:, s * heads : (s + 1) * heads] = by_head[1:2]


def gather(n, factor, *results):
    heads = results[5].shape[1]
    vmem = pl.BlockSpec(memory_space=pltpu.VMEM)
    skip = jax.ShapeDtypeStruct((1, n * heads), F32)
    return pl.pallas_call(
        functools.partial(gather_kernel, n, factor),
        out_shape=tuple(jax.ShapeDtypeStruct(one.shape, one.dtype) for one in results[:7]) + (skip, skip),
        in_specs=[vmem] * 8,
        out_specs=[vmem] * 9,
        name="gather",
    )(*results)


def on_device(n, clips, u, w1, r1, g1, k1, w2, r2, g2, k2, o1, o2, ct):
    length, features = u.shape[1:]
    head_count = k1.shape[0]
    size = features // head_count
    heads = head_count // n

    def by_device(g):
        return g.reshape(n, heads, length)

    results = whole(
        n,
        clips,
        size,
        u[0],
        w1[0],
        r1[0],
        by_device(g1),
        k1,
        w2[0],
        r2[0],
        by_device(g2),
        k2,
        o1[None],
        o2[None],
        ct[0],
    )
    factor = 1.0 / math.sqrt(clips * n * length * size)
    du, dw1, dr1, dw2, dr2, dg1, dg2, dk1, dk2 = gather(n, factor, *results)
    return (
        du[None],
        dw1[None],
        dr1[None],
        dg1.reshape(1, head_count, length),
        dk1[0],
        dw2[None],
        dr2[None],
        dg2.reshape(1, head_count, length),
        dk2[0],
    )


def solution(mesh):
    tokens, decay = P("dp", "seq", None), P("dp", None, "seq")
    return jax.shard_map(
        functools.partial(on_device, mesh.shape["seq"], mesh.shape["dp"]),
        mesh=mesh,
        in_specs=(tokens, tokens, tokens, decay, P(), tokens, tokens, decay, P(), P("seq"), P("seq"), tokens),
        out_specs=(tokens, tokens, tokens, decay, P(), tokens, tokens, decay, P()),
        check_vma=False,
    )
```

time: 56.1 us -> 42.5 us (0.76)
  Pallas kernels: 55.3 us -> 41.7 us
    pallas_call x2, Pallas kernels: 55.3 us -> 41.7 us  [the longest x1 39.2 us: whole(): pl.pallas_call(functools.partial(whole_kernel, n, clips, size, tuple(scra...]
where the time goes in v1:
time: 42.5 us; the launch traced here: 42.4 us
  Pallas kernels  41.7 us (98%)
  between operations  0.65 us (2%)
    pallas_call x1, Pallas kernels, whole(): pl.pallas_call(functools.partial(whole_kernel, n, clips, size, tuple(scra...  39.2 us
    pallas_call x1, Pallas kernels, gather(): pl.pallas_call(functools.partial(gather_kernel, n, factor), out_shape=tup...  2.52 us

profile of v1, /device:TPU:0, one launch (start us, length us, event | category | flops | bytes accessed | tf_op | source)
XLA Modules:
  0.0 42.4 jit_solution(9527572679962323984)
XLA Ops:
  0.6 39.2 %whole.1 = (bf16[128,2048]{1,0:T(8,128)(2,1)}, bf16[128,128]{1,0:T(8,128)(2,1)}, bf16[128,128]{1,0:T(8,128)(2,1)}, bf16[128,128]{1,0:T(8,128)(2,1)}, bf16[128,12...) custom-call(bf16[128,2048]{1,0:T(8,128)(2,1)} %bitcast.20, ...), custom_call_target="tpu_custom_call" | custom-call | tf_op jit(solution)/shard_map/whole/pallas_call | solution.py:516
  39.8 2.5 %gather.1 = (bf16[128,2048]{1,0:T(8,128)(2,1)}, bf16[128,128]{1,0:T(8,128)(2,1)}, bf16[128,128]{1,0:T(8,128)(2,1)}, bf16[128,128]{1,0:T(8,128)(2,1)}, bf16[128,1...) custom-call(bf16[128,2048]{1,0:T(8,128)(2,1)} %get-tuple-element.26.refs, ...), custom_call_target="tpu_custom_call" | custom-call | tf_op jit(solution)/shard_map/gather/pallas_call | solution.py:547

commit v2 on v1

--- a/solution.py
+++ b/solution.py
@@ -74,21 +74,12 @@
     return two(jnp.where(row > col if lower else row < col, scores, 0.0))
 
 
-def lead(left, scores, low, start, first, second, starts_low=None, parts_low=None):
-    both = rows_of(first, second)
-    out = nn(jnp.concatenate([left, scores], axis=1), rows_of(start, both))
-    if low is not None:
-        out = out + nn(low, both)
-    if starts_low is not None:
-        out = out + nn(jnp.concatenate([left, scores], axis=1), rows_of(starts_low, *parts_low))
-    return out
-
-
 def whole_kernel(n, clips, size, held, sems, *refs):
     x = types.SimpleNamespace(**dict(zip(held, refs[20:])))
     x.u, x.w1, x.r1, x.g1, x.k1, x.w2, x.r2, x.g2, x.k2, x.o1, x.o2, x.ct = refs[:12]
     x.dinput, x.dw1, x.dr1, x.dw2, x.dr2, x.decays1_in, x.decays2_in, x.parts_in = refs[12:20]
-    x.__dict__.update(zip(sems, zip(refs[20 + len(held) :: 2], refs[21 + len(held) :: 2])))
+    x.load, x.rounds = refs[-2:]
+    x.__dict__.update(zip(sems, zip(refs[20 + len(held) : -2 : 2], refs[21 + len(held) : -2 : 2])))
     me, clip = lax.axis_index("seq"), lax.axis_index("dp")
     chips = n // 2
     chip, core = lax.div(me, 2), lax.rem(me, 2)
@@ -101,13 +92,40 @@
     def chunk(b):
         return pl.ds(pl.multiple_of(b * length, length), length)
 
+    def cut(ref, at):
+        return ref.at[:, pl.ds(pl.multiple_of(at * features, features), features)]
+
     barrier = pltpu.get_barrier_semaphore()
     for d in range(1, n):
         pl.semaphore_signal(barrier, inc=1, device_id={"seq": lax.rem(me + d, n)}, device_id_type=MESH)
-    for d in range(1, clips):
-        pl.semaphore_signal(barrier, inc=1, device_id={"dp": lax.rem(clip + d, clips)}, device_id_type=MESH)
-    x.ct_out[...] = x.ct[...].astype(BF16)
-    pl.semaphore_wait(barrier, n + clips - 2)
+    lines = ((clip >= 0, clip + 1 - 2 * lax.rem(clip, 2)), (clip >= 2, clip - 2), (clip < clips - 2, clip + 2))
+    greetings = sum(jnp.where(there, 1, 0) for there, _ in lines)
+
+    def greet(sem):
+        for there, to in lines:
+
+            @pl.when(there)
+            def _():
+                pl.semaphore_signal(sem, inc=1, device_id={"dp": to}, device_id_type=MESH)
+
+    met = []
+
+    def hear(count):
+        for k in range(len(met), count):
+            pl.semaphore_wait(x.rounds.at[k], greetings)
+            met.append(k)
+            if k + 1 < clips // 2 - 1:
+                greet(x.rounds.at[k + 1])
+
+    greet(barrier)
+    load = pltpu.make_async_copy(x.ct, x.ct_wide, x.load.at[0])
+    load.start()
+    own_load = pltpu.make_async_copy(cut(x.u, me), x.u_all.at[me], x.load.at[1])
+    own_load.start()
+    load.wait()
+    x.ct_out[...] = x.ct_wide[...].astype(BF16)
+    pl.semaphore_wait(barrier, n - 1 + greetings)
+    greet(x.rounds.at[0])
 
     def copy_to(axis, to, src, dst, pair, *at):
         return pltpu.make_async_remote_copy(
@@ -119,16 +137,13 @@
             device_id_type=MESH,
         )
 
-    def cut(ref, at):
-        return ref.at[:, pl.ds(pl.multiple_of(at * features, features), features)]
-
     def device(away, other):
         return 2 * lax.rem(chip + away, chips) + (1 - core if other else core)
 
     peers = [(away, other) for away in range(1, chips) for other in (0, 1)] + [(0, 1)]
     moves = [
         lambda to: (x.g2.at[to], x.g_all.at[1, me]),
-        lambda to: (cut(x.ct_out, to), x.ct_all.at[me]),
+        lambda to: (cut(x.ct_out, to), x.ct_all.at[chunk(me)]),
         lambda to: (x.g1.at[to], x.g_all.at[0, me]),
         lambda to: (cut(x.u, to), x.u_all.at[me]),
         lambda to: (x.o1, x.o1_all.at[me]),
@@ -155,6 +170,12 @@
         copy = copy_to("seq", twin, src, dst.at[me], x.near, chips - 1, k)
         copy.start()
         near.append(copy)
+
+    def wait_block(k, b):
+        away = lax.rem(chip - lax.div(b, 2) + chips, chips)
+        at = 2 * away + lax.rem(core + lax.rem(b, 2), 2) - 1
+        src, dst = moves[k](b)
+        copy_to("seq", b, src, dst, x.move, at, k).wait_recv()
 
     def wait_for(k):
         for copy in arriving[k]:
@@ -174,8 +195,7 @@
     x.g_all[1, me] = x.g2[me]
     for src, dst in pairs + ((x.o1, x.o1_all), (x.o2, x.o2_all)):
         dst[me] = src[...]
-    x.u_all[me] = x.u[:, here]
-    x.ct_all[me] = x.ct_out[:, here]
+    x.ct_all[chunk(me)] = x.ct_out[:, here]
 
     first = me * heads
 
@@ -196,7 +216,7 @@
             x.sums[layer, b] = sums
             return carry
 
-        lax.fori_loop(0, n, step, 0)
+        lax.fori_loop(0, n, step, 0, unroll=4)
 
     def prepare_scores(layer):
         def step(b, carry):
@@ -205,7 +225,7 @@
             x.back[layer, b], x.back_low[layer, b] = strict_scores(w, r, False)
             return carry
 
-        lax.fori_loop(0, n, step, 0)
+        lax.fori_loop(0, n, step, 0, unroll=4)
 
     def prepare_order(src, dst, out):
         def step(i, carry):
@@ -213,9 +233,10 @@
             out[i] = jnp.concatenate([(cell == src[j].astype(F32)).astype(BF16) for j in range(n)], axis=1)
             return carry
 
-        lax.fori_loop(0, n, step, 0)
+        lax.fori_loop(0, n, step, 0, unroll=4)
 
     wait_for(0)
+    hear(1)
     prepare_decays(1)
     wait_for(2)
     prepare_decays(0)
@@ -242,78 +263,104 @@
     def own(w, r):
         return jnp.sum(w.astype(F32) * r.astype(F32), axis=1, keepdims=True)
 
-    def back(layer, b, dy):
-        wide, w, r = dy.astype(F32), x.w_all[layer, b], x.r_all[layer, b]
-        sums, scores, low = x.sums[layer, b], x.back[layer, b], x.back_low[layer, b]
-        scaled = wide * x.grown[layer, b]
-        high = scaled.astype(BF16)
-        a, z = high[:half], high[half:]
-        turned = (scaled[half:] * sums[5:6]).astype(BF16)
-        end = adjoint[...]
-        end_a, end_z = (end * sums[2:3]).astype(BF16), (end * sums[3:4]).astype(BF16)
-        x.ends[layer, b] = end
-        x.ends_a[layer, b] = end_a
-        x.ends_z[layer, b] = end_z
-        x.dys[layer, b] = high
-        top = lead(w[:half], scores[:half], low[:half], end_a, a, turned)
-        bottom = lead(w[half:], scores[half:], low[half:], end_z, a, z)
-        inner = rows_of(top, bottom) * x.shrunk[layer, b]
-        x.inner[layer, b] = inner
-        carried = rows_of(scaled[:half] * sums[0:1], scaled[half:] * sums[1:2]).astype(BF16)
-        adjoint[...] = end * sums[4:5] + tn(r, carried)
-        return inner + (skips[layer] + own(w, r)) * wide
+    step = min(2 * length, features)
+    tiles = [slice(at, at + step) for at in range(0, features, step)]
+
+    def back(layer, b, get, put):
+        w, r = x.w_all[layer, b], x.r_all[layer, b]
+        scores, low = x.back[layer, b], x.back_low[layer, b]
+        left_a = jnp.concatenate([w[:half], scores[:half]], axis=1)
+        left_z = jnp.concatenate([w[half:], scores[half:]], axis=1)
+        diagonal = own(w, r)
+        for lanes in tiles:
+            wide, sums = get(lanes).astype(F32), x.sums[layer, b, :, lanes]
+            scaled = wide * x.grown[layer, b, :, lanes]
+            high = scaled.astype(BF16)
+            a, z = high[:half], high[half:]
+            x.dys[layer, b, :, lanes] = high
+            turned = (scaled[half:] * sums[5:6]).astype(BF16)
+            end = adjoint[:, lanes]
+            carried = rows_of(scaled[:half] * sums[0:1], scaled[half:] * sums[1:2]).astype(BF16)
+            adjoint[:, lanes] = end * sums[4:5] + tn(r, carried)
+            end_a, end_z = (end * sums[2:3]).astype(BF16), (end * sums[3:4]).astype(BF16)
+            x.ends[layer, b, :, lanes] = end
+            x.ends_a[layer, b, :, lanes] = end_a
+            x.ends_z[layer, b, :, lanes] = end_z
+            top = nn(left_a, rows_of(end_a, a, turned)) + nn(low[:half], rows_of(a, turned))
+            bottom = nn(left_z, rows_of(end_z, a, z)) + nn(low[half:], high)
+            inner = rows_of(top, bottom) * x.shrunk[layer, b, :, lanes]
+            x.inner[layer, b, :, lanes] = inner
+            put(lanes, (inner + (skips[layer][:, lanes] + diagonal) * wide).astype(BF16))
 
     lower = iota((length, length), 0) >= iota((length, length), 1)
     since = lower.astype(BF16)
     picks = (iota((features, heads), 0) // size == iota((features, heads), 1)).astype(BF16)
 
-    def forward(layer, b, u, dy, precise):
-        wide, wide_dy, w, r = u.astype(F32), dy.astype(F32), x.w_all[layer, b], x.r_all[layer, b]
-        sums, scores, low = x.sums[layer, b], x.fore[layer, b], x.fore_low[layer, b]
-        scaled = wide * x.shrunk[layer, b]
-        high, rest = two(scaled)
-        a, z, a_low, z_low = high[:half], high[half:], rest[:half], rest[half:]
-        turned, turned_low = two(scaled[:half] * sums[5:6])
-        start = state[...]
-        start_a, start_a_low = two(start * sums[0:1])
-        start_z, start_z_low = two(start * sums[1:2])
-        if precise:
-            top = lead(r[:half], scores[:half], low[:half], start_a, a, z, start_a_low, (a_low, z_low))
-            bottom = lead(r[half:], scores[half:], low[half:], start_z, turned, z, start_z_low, (turned_low, z_low))
-        else:
-            top = lead(r[:half], scores[:half], None, start_a, a, z)
-            bottom = lead(r[half:], scores[half:], None, start_z, turned, z)
-        inner = rows_of(top, bottom) * x.grown[layer, b]
-        carried, carried_low = two(rows_of(scaled[:half] * sums[2:3], scaled[half:] * sums[3:4]))
-        after = start * sums[4:5] + tn(w, carried)
-        if precise:
-            after = after + tn(w, carried_low)
-        state[...] = after
-
-        through = jnp.sum(x.ends[layer, b] * after, axis=0, keepdims=True)
-        terms = wide_dy * inner - wide * x.inner[layer, b]
-        last = terms[length - 8 :] + jnp.where(iota((8, features), 0) == 7, through, 0.0)
-        terms, terms_low = two(rows_of(terms[: length - 8], last))
-        by_head, by_head_low = two(nn(terms, picks) + nn(terms_low, picks))
-        ddecay = tn(by_head, since) + tn(by_head_low, since)
-
-        dys = x.dys[layer, b]
-        dy_a, dy_z = dys[:half], dys[half:]
-        dscores = rows_of(
-            nt(dy_a, high) + nt(dy_a, rest),
-            nt(dy_z, rows_of(turned, z)) + nt(dy_z, rows_of(turned_low, z_low)),
-        )
-        dscores, dscores_low = two(jnp.where(lower, dscores, 0.0))
-        dreads = nn(dscores, w) + nn(dscores_low, w) + rows_of(nt(dy_a, start_a), nt(dy_z, start_z))
-        dwrites = (
-            tn(dscores, r)
-            + tn(dscores_low, r)
-            + rows_of(nt(a, x.ends_a[layer, b]), nt(z, x.ends_z[layer, b]))
-        )
-        x.params[layer, b, 0] = dwrites
-        x.params[layer, b, 1] = dreads
-        x.decays[layer, b] = ddecay
-        return inner + (skips[layer] + own(w, r)) * wide
+    def forward(layer, b, get, put):
+        w, r = x.w_all[layer, b], x.r_all[layer, b]
+        scores, low = x.fore[layer, b], x.fore_low[layer, b]
+        left_a = jnp.concatenate([r[:half], scores[:half]], axis=1)
+        left_z = jnp.concatenate([r[half:], scores[half:]], axis=1)
+        diagonal = own(w, r)
+        for lanes in tiles:
+            wide, sums = get(lanes).astype(F32), x.sums[layer, b, :, lanes]
+            scaled = wide * x.shrunk[layer, b, :, lanes]
+            high, rest = two(scaled)
+            turned, turned_low = two(scaled[:half] * sums[5:6])
+            start = state[:, lanes]
+            carried, carried_low = two(rows_of(scaled[:half] * sums[2:3], scaled[half:] * sums[3:4]))
+            after = start * sums[4:5] + tn(w, carried)
+            if put:
+                after = after + tn(w, carried_low)
+            state[:, lanes] = after
+            start_a, start_a_low = two(start * sums[0:1])
+            start_z, start_z_low = two(start * sums[1:2])
+            other, other_low = rows_of(turned, high[half:]), rows_of(turned_low, rest[half:])
+            top = nn(left_a, rows_of(start_a, high))
+            bottom = nn(left_z, rows_of(start_z, other))
+            if put:
+                top = top + nn(low[:half], high) + nn(left_a, rows_of(start_a_low, rest))
+                bottom = bottom + nn(low[half:], other) + nn(left_z, rows_of(start_z_low, other_low))
+            inner = rows_of(top, bottom) * x.grown[layer, b, :, lanes]
+            if put:
+                put(lanes, wide, (inner + (skips[layer][:, lanes] + diagonal) * wide).astype(BF16))
+            x.us[layer, b, 0, :, lanes] = high
+            x.us[layer, b, 1, :, lanes] = rest
+            x.turns[layer, b, 0, :, lanes] = turned
+            x.turns[layer, b, 1, :, lanes] = turned_low
+            x.starts_a[layer, b, :, lanes] = start_a
+            x.starts_z[layer, b, :, lanes] = start_z
+            x.through[layer, b, :, lanes] = jnp.sum(x.ends[layer, b, :, lanes] * after, axis=0, keepdims=True)
+            x.outer[layer, b, :, lanes] = inner
+
+    def grads(layer, b, get, get_dy):
+        w, r = x.w_all[layer, b], x.r_all[layer, b]
+        totals = []
+        for lanes in tiles:
+            wide, wide_dy = get(lanes).astype(F32), get_dy(lanes).astype(F32)
+            terms = wide_dy * x.outer[layer, b, :, lanes] - wide * x.inner[layer, b, :, lanes]
+            through = jnp.where(iota((8, step), 0) == 7, x.through[layer, b, :, lanes], 0.0)
+            terms, terms_low = two(rows_of(terms[: length - 8], terms[length - 8 :] + through))
+            high, rest = x.us[layer, b, 0, :, lanes], x.us[layer, b, 1, :, lanes]
+            other = rows_of(x.turns[layer, b, 0, :, lanes], high[half:])
+            other_low = rows_of(x.turns[layer, b, 1, :, lanes], rest[half:])
+            dys = x.dys[layer, b, :, lanes]
+            dy_a, dy_z = dys[:half], dys[half:]
+            parts = (
+                nn(terms, picks[lanes]) + nn(terms_low, picks[lanes]),
+                nt(dy_a, high) + nt(dy_a, rest),
+                nt(dy_z, other) + nt(dy_z, other_low),
+                nt(dy_a, x.starts_a[layer, b, :, lanes]),
+                nt(dy_z, x.starts_z[layer, b, :, lanes]),
+                nt(high[:half], x.ends_a[layer, b, :, lanes]),
+                nt(high[half:], x.ends_z[layer, b, :, lanes]),
+            )
+            totals = [one + part for one, part in zip(totals, parts)] if totals else parts
+        by_head, by_head_low = two(totals[0])
+        x.decays[layer, b] = tn(by_head, since) + tn(by_head_low, since)
+        dscores, dscores_low = two(jnp.where(lower, rows_of(*totals[1:3]), 0.0))
+        x.params[layer, b, 0] = tn(dscores, r) + tn(dscores_low, r) + rows_of(*totals[5:7])
+        x.params[layer, b, 1] = nn(dscores, w) + nn(dscores_low, w) + rows_of(*totals[3:5])
 
     decays_in = (x.decays1_in, x.decays2_in)
 
@@ -352,25 +399,38 @@
             copy.start()
             chip_copies.append(copy)
 
-    wait_for(1)
+    hear(2)
 
     def back_second(i, carry):
         b = n - 1 - i
-        x.du2[chunk(b)] = back(1, b, x.ct_all[b]).astype(BF16)
+
+        @pl.when(b != me)
+        def _():
+            wait_block(1, b)
+
+        def put(lanes, value):
+            x.du2[chunk(b), lanes] = value
+
+        back(1, b, lambda lanes: x.ct_all[chunk(b), lanes], put)
         return carry
 
-    lax.fori_loop(0, n, back_second, 0, unroll=2)
+    lax.fori_loop(0, n, back_second, 0, unroll=4)
 
     def regrid_back(i, carry):
         x.dy1[chunk(i)] = nn(x.take_first[i], x.du2[...]).astype(BF16)
+        x.ct_first[chunk(i)] = nn(x.take_first[i], x.ct_all[...]).astype(BF16)
         return carry
 
-    lax.fori_loop(0, n, regrid_back, 0, unroll=2)
+    lax.fori_loop(0, n, regrid_back, 0, unroll=4)
     adjoint[...] = jnp.zeros_like(adjoint)
 
     def back_first(i, carry):
         b = n - 1 - i
-        x.du1[b] = back(0, b, x.dy1[chunk(b)]).astype(BF16)
+
+        def put(lanes, value):
+            x.du1[b, :, lanes] = value
+
+        back(0, b, lambda lanes: x.dy1[chunk(b), lanes], put)
 
         @pl.when(b != me)
         def _():
@@ -378,26 +438,26 @@
 
         return carry
 
-    lax.fori_loop(0, n, back_first, 0)
-    wait_for(3)
+    lax.fori_loop(0, n, back_first, 0, unroll=4)
+    own_load.wait()
+    hear(clips // 2 - 1)
     x.skips[...] = jnp.zeros_like(x.skips)
 
     def first_layer(b, carry):
-        u, dy = x.u_all[b], x.dy1[chunk(b)]
-        x.y1[chunk(b)] = forward(0, b, u, dy, True).astype(BF16)
-        x.skips[0:1, :] += jnp.sum(u.astype(F32) * dy.astype(F32), axis=0, keepdims=True)
-        leave(0, b)
+        @pl.when(b != me)
+        def _():
+            wait_block(3, b)
+
+        def put(lanes, wide, value):
+            x.y1[chunk(b), lanes] = value
+            x.skips[0:1, lanes] += jnp.sum(wide * x.dy1[chunk(b), lanes].astype(F32), axis=0, keepdims=True)
+            upstream = x.ct_first[chunk(b), lanes].astype(F32)
+            x.skips[1:2, lanes] += jnp.sum(value.astype(F32) * upstream, axis=0, keepdims=True)
+
+        forward(0, b, lambda lanes: x.u_all[b, :, lanes], put)
         return carry
 
-    lax.fori_loop(0, n, first_layer, 0)
-
-    def regrid(i, carry):
-        u = nn(x.take_second[i], x.y1[...])
-        x.u2[i] = u.astype(BF16)
-        x.skips[1:2, :] += jnp.sum(u * x.ct_all[i].astype(F32), axis=0, keepdims=True)
-        return carry
-
-    lax.fori_loop(0, n, regrid, 0, unroll=2)
+    lax.fori_loop(0, n, first_layer, 0, unroll=4)
     clip_copies = []
     for d in range(1, clips):
         to = lax.rem(clip + d, clips)
@@ -405,15 +465,29 @@
         copy.start()
         clip_copies.append(copy)
     x.clips_in[clip] = x.skips[...]
+
+    def first_grads(b, carry):
+        grads(0, b, lambda lanes: x.u_all[b, :, lanes], lambda lanes: x.dy1[chunk(b), lanes])
+        leave(0, b)
+        return carry
+
+    lax.fori_loop(0, n, first_grads, 0, unroll=4)
+
+    def regrid(i, carry):
+        x.u2[i] = nn(x.take_second[i], x.y1[...]).astype(BF16)
+        return carry
+
+    lax.fori_loop(0, n, regrid, 0, unroll=4)
     leave_chip(0)
     state[...] = jnp.zeros_like(state)
 
     def second_layer(b, carry):
-        forward(1, b, x.u2[b], x.ct_all[b], False)
+        forward(1, b, lambda lanes: x.u2[b, :, lanes], None)
+        grads(1, b, lambda lanes: x.u2[b, :, lanes], lambda lanes: x.ct_all[chunk(b), lanes])
         leave(1, b)
         return carry
 
-    lax.fori_loop(0, n, second_layer, 0)
+    lax.fori_loop(0, n, second_layer, 0, unroll=4)
     for copy in clip_copies:
         copy.wait()
     x.summed[...] = jnp.sum(x.clips_in[...], axis=0)
@@ -460,14 +534,17 @@
     features, half, chips = heads * size, length // 2, n // 2
     vmem = pl.BlockSpec(memory_space=pltpu.VMEM)
     smem = pl.BlockSpec(memory_space=pltpu.SMEM)
+    away = pl.BlockSpec(memory_space=pl.ANY)
     param, decay, gain = (length, count), (n, heads, length), (2, features)
     wide, flat, held, square = (n, length, features), (n * length, features), (n, count, features), (n, length, length)
     order, pick, pair = (n, 1, length), (n, length, n * length), (2, length, count)
     outs = (((length, width), BF16),) + ((param, BF16),) * 4 + ((decay, F32),) * 2 + (((n,) + gain, F32),)
     scratch = dict(
         ct_out=((length, width), BF16),
+        ct_wide=((length, width), F32),
         u_all=(wide, BF16),
-        ct_all=(wide, BF16),
+        ct_all=(flat, BF16),
+        ct_first=(flat, BF16),
         w_all=((2, n) + param, BF16),
         r_all=((2, n) + param, BF16),
         g_all=((2,) + decay, F32),
@@ -492,6 +569,12 @@
         ends_a=((2,) + held, BF16),
         ends_z=((2,) + held, BF16),
         inner=((2,) + wide, F32),
+        outer=((2,) + wide, F32),
+        us=((2, n, 2, length, features), BF16),
+        turns=((2, n, 2, half, features), BF16),
+        starts_a=((2,) + held, BF16),
+        starts_z=((2,) + held, BF16),
+        through=((2, n, 1, features), F32),
         state=((count, features), F32),
         adjoint=((count, features), F32),
         params=((2, n) + pair, F32),
@@ -513,14 +596,18 @@
         clip=(clips - 1,),
         part=(n - 1,),
     )
+    taken = sum(math.prod(shape) * jnp.dtype(kind).itemsize for shape, kind in scratch.values())
     return pl.pallas_call(
         functools.partial(whole_kernel, n, clips, size, tuple(scratch), tuple(sems)),
         out_shape=tuple(jax.ShapeDtypeStruct(*out) for out in outs),
-        in_specs=[vmem] * 4 + [smem] + [vmem] * 3 + [smem] + [vmem] * 3,
+        in_specs=[away] + [vmem] * 3 + [smem] + [vmem] * 3 + [smem] + [vmem] * 2 + [away],
         out_specs=[vmem] * 8,
         scratch_shapes=[pltpu.VMEM(*one) for one in scratch.values()]
-        + [pltpu.SemaphoreType.DMA(shape) for shape in sems.values() for _ in range(2)],
-        compiler_params=pltpu.CompilerParams(collective_id=0, has_side_effects=True),
+        + [pltpu.SemaphoreType.DMA(shape) for shape in sems.values() for _ in range(2)]
+        + [pltpu.SemaphoreType.DMA((2,)), pltpu.SemaphoreType.REGULAR((clips // 2 - 1,))],
+        compiler_params=pltpu.CompilerParams(
+            collective_id=0, has_side_effects=True
+        ),
         name="whole",
     )(*args)
 

time: 42.5 us -> 36.5 us (0.86)
  Pallas kernels: 41.7 us -> 35.6 us
    pallas_call x1, Pallas kernels: 39.2 us -> 33.1 us  [whole(): pl.pallas_call(functools.partial(whole_kernel, n, clips, size, tuple(scra...]
where the time goes in v2:
time: 36.5 us; the launch traced here: 36.3 us
  Pallas kernels  35.6 us (98%)
  between operations  0.65 us (2%)
    pallas_call x1, Pallas kernels, whole(): pl.pallas_call(functools.partial(whole_kernel, n, clips, size, tuple(scra...  33.1 us
    pallas_call x1, Pallas kernels, gather(): pl.pallas_call(functools.partial(gather_kernel, n, factor), out_shape=tup...  2.52 us

profile of v2, /device:TPU:0, one launch (start us, length us, event | category | flops | bytes accessed | tf_op | source)
XLA Modules:
  0.0 36.3 jit_solution(6878804187887521442)
XLA Ops:
  0.6 33.1 %whole.1 = (bf16[128,2048]{1,0:T(8,128)(2,1)}, bf16[128,128]{1,0:T(8,128)(2,1)}, bf16[128,128]{1,0:T(8,128)(2,1)}, bf16[128,128]{1,0:T(8,128)(2,1)}, bf16[128,12...) custom-call(bf16[128,2048]{1,0:T(8,128)(2,1)} %bitcast.20, ...), custom_call_target="tpu_custom_call" | custom-call | tf_op jit(solution)/shard_map/whole/pallas_call | solution.py:600
  33.7 2.5 %gather.1 = (bf16[128,2048]{1,0:T(8,128)(2,1)}, bf16[128,128]{1,0:T(8,128)(2,1)}, bf16[128,128]{1,0:T(8,128)(2,1)}, bf16[128,128]{1,0:T(8,128)(2,1)}, bf16[128,1...) custom-call(bf16[128,2048]{1,0:T(8,128)(2,1)} %get-tuple-element.26.refs, ...), custom_call_target="tpu_custom_call" | custom-call | tf_op jit(solution)/shard_map/gather/pallas_call | solution.py:634

commit v3 on v2

v3 whole, which is shorter than its diff:
```python
import functools
import math
import types

import jax
import jax.numpy as jnp
from jax import lax
from jax.experimental import pallas as pl
from jax.experimental.pallas import tpu as pltpu
from jax.sharding import PartitionSpec as P

MESH = pl.DeviceIdType.MESH
HIGHEST = lax.Precision.HIGHEST
F32 = jnp.float32
BF16 = jnp.bfloat16


def nn(a, b, precision=None):
    return lax.dot_general(a, b, (((1,), (0,)), ((), ())), precision=precision, preferred_element_type=F32)


def nt(a, b, precision=None):
    return lax.dot_general(a, b, (((1,), (1,)), ((), ())), precision=precision, preferred_element_type=F32)


def tn(a, b, precision=None):
    return lax.dot_general(a, b, (((0,), (0,)), ((), ())), precision=precision, preferred_element_type=F32)


def iota(shape, dim):
    return lax.broadcasted_iota(jnp.int32, shape, dim)


def two(a):
    high = a.astype(BF16)
    return high, (a - high.astype(F32)).astype(BF16)


def rows_of(*parts):
    return jnp.concatenate(parts, axis=0)


def decay_sums(length):
    half, mid = length // 2, length // 4
    t, s = iota((length + 8, length), 0), iota((length + 8, length), 1)
    first, second = mid, half + mid
    middle = jnp.where(t < half, first, second)
    by_token = (s <= t).astype(F32) - (s < middle).astype(F32)
    k = t - length
    by_chunk = jnp.where(k == 0, (s < first).astype(F32), 0.0)
    by_chunk = jnp.where(k == 1, (s < second).astype(F32), by_chunk)
    by_chunk = jnp.where(k == 2, (s >= first).astype(F32), by_chunk)
    by_chunk = jnp.where(k == 3, (s >= second).astype(F32), by_chunk)
    by_chunk = jnp.where(k == 4, 1.0, by_chunk)
    by_chunk = jnp.where(k == 5, ((s >= first) & (s < second)).astype(F32), by_chunk)
    return jnp.where(k < 0, by_token, by_chunk).astype(BF16)


def factors(log_decay, size):
    heads, length = log_decay.shape
    sums = decay_sums(length)
    wide = [
        jnp.concatenate([jnp.broadcast_to(part[h : h + 1], (size, length)) for h in range(heads)], axis=0).astype(BF16)
        for part in (p.astype(F32) for p in two(log_decay))
    ]
    logs = nt(sums, wide[0]) + nt(sums, wide[1])
    by_token = logs[:length]
    return jnp.exp(by_token), jnp.exp(-by_token), jnp.exp(logs[length:])


def strict_scores(a, b, lower):
    scores = nt(a, b)
    row, col = iota(scores.shape, 0), iota(scores.shape, 1)
    return two(jnp.where(row > col if lower else row < col, scores, 0.0))


def whole_kernel(n, clips, size, factor, held, sems, *refs):
    x = types.SimpleNamespace(**dict(zip(held, refs[21:])))
    x.u, x.w1, x.r1, x.g1, x.k1, x.w2, x.r2, x.g2, x.k2, x.o1, x.o2, x.ct = refs[:12]
    x.dinput, x.dw1, x.dr1, x.dw2, x.dr2, x.decays1_in, x.decays2_in, x.dk1, x.dk2 = refs[12:21]
    x.load, x.rounds = refs[-2:]
    x.__dict__.update(zip(sems, zip(refs[21 + len(held) : -2 : 2], refs[22 + len(held) : -2 : 2])))
    me, clip = lax.axis_index("seq"), lax.axis_index("dp")
    chips = n // 2
    chip, core = lax.div(me, 2), lax.rem(me, 2)
    twin = me + 1 - 2 * core
    heads, length = x.g1.shape[1:]
    features = heads * size
    half = length // 2
    here = pl.ds(pl.multiple_of(me * features, features), features)

    def chunk(b):
        return pl.ds(pl.multiple_of(b * length, length), length)

    def cut(ref, at):
        return ref.at[:, pl.ds(pl.multiple_of(at * features, features), features)]

    barrier = pltpu.get_barrier_semaphore()
    for d in range(1, n):
        pl.semaphore_signal(barrier, inc=1, device_id={"seq": lax.rem(me + d, n)}, device_id_type=MESH)
    lines = ((clip >= 0, clip + 1 - 2 * lax.rem(clip, 2)), (clip >= 2, clip - 2), (clip < clips - 2, clip + 2))
    greetings = sum(jnp.where(there, 1, 0) for there, _ in lines)

    def greet(sem):
        for there, to in lines:

            @pl.when(there)
            def _():
                pl.semaphore_signal(sem, inc=1, device_id={"dp": to}, device_id_type=MESH)

    met = []

    def hear(count):
        for k in range(len(met), count):
            pl.semaphore_wait(x.rounds.at[k], greetings)
            met.append(k)
            if k + 1 < clips // 2 - 1:
                greet(x.rounds.at[k + 1])

    greet(barrier)
    load = pltpu.make_async_copy(x.ct, x.ct_wide, x.load.at[0])
    load.start()
    own_load = pltpu.make_async_copy(cut(x.u, me), x.u_all.at[me], x.load.at[1])
    own_load.start()
    load.wait()
    x.ct_out[...] = x.ct_wide[...].astype(BF16)
    pl.semaphore_wait(barrier, n - 1 + greetings)
    greet(x.rounds.at[0])

    def copy_to(axis, to, src, dst, pair, *at):
        return pltpu.make_async_remote_copy(
            src_ref=src,
            dst_ref=dst,
            send_sem=pair[0].at[at],
            recv_sem=pair[1].at[at],
            device_id={axis: to},
            device_id_type=MESH,
        )

    def device(away, other):
        return 2 * lax.rem(chip + away, chips) + (1 - core if other else core)

    peers = [(away, other) for away in range(1, chips) for other in (0, 1)] + [(0, 1)]
    moves = [
        lambda to: (x.g2.at[to], x.g_all.at[1, me]),
        lambda to: (x.g1.at[to], x.g_all.at[0, me]),
        lambda to: (x.o1, x.o1_all.at[me]),
        lambda to: (x.o2, x.o2_all.at[me]),
    ]
    step = min(2 * length, features)
    tiles = [slice(at, at + step) for at in range(0, features, step)]

    def tile_moves(lanes):
        def at(to):
            return pl.ds(pl.multiple_of(to * features + lanes.start, step), step)

        return [
            lambda to: (x.ct_out.at[:, at(to)], x.ct_all.at[chunk(me), lanes]),
            lambda to: (x.u.at[:, at(to)], x.u_all.at[me, :, lanes]),
        ]

    ct_at = len(moves)
    u_at = ct_at + 1
    for lanes in tiles:
        moves += tile_moves(lanes)
    arriving = [[] for _ in moves]

    def issue(k):
        for away, other in peers:
            to = device(away, other)
            copy = copy_to("seq", to, *moves[k](to), x.move, 2 * away + other - 1, k)
            copy.start()
            arriving[k].append(copy)

    pairs = ((x.w2, x.w_all.at[1]), (x.r2, x.r_all.at[1]), (x.w1, x.w_all.at[0]), (x.r1, x.r_all.at[0]))
    far, near = [], []

    def issue_pair(k):
        src, dst = pairs[k]
        for away in range(1, chips):
            copy = copy_to("seq", device(away, 0), src, dst.at[me], x.near, away - 1, k)
            copy.start()
            far.append(copy)
        copy = copy_to("seq", twin, src, dst.at[me], x.near, chips - 1, k)
        copy.start()
        near.append(copy)

    def wait_for(k):
        for copy in arriving[k]:
            copy.wait_recv()

    issue_pair(0)
    issue_pair(1)
    issue(0)
    issue(1)
    issue_pair(2)
    issue_pair(3)
    for k in range(2, len(moves)):
        issue(k)
    x.g_all[0, me] = x.g1[me]
    x.g_all[1, me] = x.g2[me]
    for src, dst in pairs + ((x.o1, x.o1_all), (x.o2, x.o2_all)):
        dst[me] = src[...]
    x.ct_all[chunk(me)] = x.ct_out[:, here]

    first = me * heads

    def gains(ref):
        channel = iota((1, features), 1) // size
        row = jnp.zeros((1, features), F32)
        for h in range(heads):
            row = jnp.where(channel == h, ref[first + h], row)
        return row

    skips = (gains(x.k1), gains(x.k2))

    def prepare_decays(layer):
        def step(b, carry):
            grown, shrunk, sums = factors(x.g_all[layer, b], size)
            x.grown[layer, b] = grown
            x.shrunk[layer, b] = shrunk
            x.sums[layer, b] = sums
            return carry

        lax.fori_loop(0, n, step, 0, unroll=4)

    def prepare_scores(layer):
        def step(b, carry):
            w, r = x.w_all[layer, b], x.r_all[layer, b]
            x.fore[layer, b], x.fore_low[layer, b] = strict_scores(r, w, True)
            x.back[layer, b], x.back_low[layer, b] = strict_scores(w, r, False)
            return carry

        lax.fori_loop(0, n, step, 0, unroll=4)

    def prepare_order(src, dst, out):
        def step(i, carry):
            cell = jnp.transpose(jnp.broadcast_to(dst[i].astype(F32), (length, length)))
            out[i] = jnp.concatenate([(cell == src[j].astype(F32)).astype(BF16) for j in range(n)], axis=1)
            return carry

        lax.fori_loop(0, n, step, 0, unroll=4)

    wait_for(0)
    hear(1)
    prepare_decays(1)
    wait_for(1)
    prepare_decays(0)
    for copy in far:
        copy.wait_recv()
    for k, (src, dst) in enumerate(pairs):
        for away in range(1, chips):
            block = 2 * lax.rem(chip - away + chips, chips) + core
            copy = copy_to("seq", twin, dst.at[block], dst.at[block], x.near, chips - 1 + away, k)
            copy.start()
            near.append(copy)
    wait_for(2)
    wait_for(3)
    prepare_order(x.o2_all, x.o1_all, x.take_first)
    prepare_order(x.o1_all, x.o2_all, x.take_second)
    for copy in near:
        copy.wait_recv()
    prepare_scores(1)
    prepare_scores(0)
    state, adjoint = x.state, x.adjoint
    adjoint[...] = jnp.zeros_like(adjoint)
    state[...] = jnp.zeros_like(state)

    def own(w, r):
        return jnp.sum(w.astype(F32) * r.astype(F32), axis=1, keepdims=True)

    def back(layer, b, lanes, dy):
        w, r = x.w_all[layer, b], x.r_all[layer, b]
        scores, low = x.back[layer, b], x.back_low[layer, b]
        left_a = jnp.concatenate([w[:half], scores[:half]], axis=1)
        left_z = jnp.concatenate([w[half:], scores[half:]], axis=1)
        wide, sums = dy.astype(F32), x.sums[layer, b, :, lanes]
        scaled = wide * x.grown[layer, b, :, lanes]
        high = scaled.astype(BF16)
        a, z = high[:half], high[half:]
        x.dys[layer, b, :, lanes] = high
        turned = (scaled[half:] * sums[5:6]).astype(BF16)
        end = adjoint[:, lanes]
        carried = rows_of(scaled[:half] * sums[0:1], scaled[half:] * sums[1:2]).astype(BF16)
        adjoint[:, lanes] = end * sums[4:5] + tn(r, carried)
        end_a, end_z = (end * sums[2:3]).astype(BF16), (end * sums[3:4]).astype(BF16)
        x.ends[layer, b, :, lanes] = end
        x.ends_a[layer, b, :, lanes] = end_a
        x.ends_z[layer, b, :, lanes] = end_z
        top = nn(left_a, rows_of(end_a, a, turned)) + nn(low[:half], rows_of(a, turned))
        bottom = nn(left_z, rows_of(end_z, a, z)) + nn(low[half:], high)
        inner = rows_of(top, bottom) * x.shrunk[layer, b, :, lanes]
        x.inner[layer, b, :, lanes] = inner
        return (inner + (skips[layer][:, lanes] + own(w, r)) * wide).astype(BF16)

    lower = iota((length, length), 0) >= iota((length, length), 1)
    since = lower.astype(BF16)
    picks = (iota((features, heads), 0) // size == iota((features, heads), 1)).astype(BF16)

    def forward(layer, b, lanes, u, put):
        w, r = x.w_all[layer, b], x.r_all[layer, b]
        scores, low = x.fore[layer, b], x.fore_low[layer, b]
        left_a = jnp.concatenate([r[:half], scores[:half]], axis=1)
        left_z = jnp.concatenate([r[half:], scores[half:]], axis=1)
        wide, sums = u.astype(F32), x.sums[layer, b, :, lanes]
        scaled = wide * x.shrunk[layer, b, :, lanes]
        high, rest = two(scaled)
        turned, turned_low = two(scaled[:half] * sums[5:6])
        start = state[:, lanes]
        carried, carried_low = two(rows_of(scaled[:half] * sums[2:3], scaled[half:] * sums[3:4]))
        after = start * sums[4:5] + tn(w, carried)
        if put:
            after = after + tn(w, carried_low)
        state[:, lanes] = after
        start_a, start_a_low = two(start * sums[0:1])
        start_z, start_z_low = two(start * sums[1:2])
        other, other_low = rows_of(turned, high[half:]), rows_of(turned_low, rest[half:])
        top = nn(left_a, rows_of(start_a, high))
        bottom = nn(left_z, rows_of(start_z, other))
        if put:
            top = top + nn(low[:half], high) + nn(left_a, rows_of(start_a_low, rest))
            bottom = bottom + nn(low[half:], other) + nn(left_z, rows_of(start_z_low, other_low))
        inner = rows_of(top, bottom) * x.grown[layer, b, :, lanes]
        if put:
            put(wide, (inner + (skips[layer][:, lanes] + own(w, r)) * wide).astype(BF16))
        x.us[layer, b, 0, :, lanes] = high
        if put:
            x.us[layer, b, 1, :, lanes] = rest
            x.turns[layer, b, 1, :, lanes] = turned_low
        x.turns[layer, b, 0, :, lanes] = turned
        x.starts_a[layer, b, :, lanes] = start_a
        x.starts_z[layer, b, :, lanes] = start_z
        x.through[layer, b, :, lanes] = jnp.sum(x.ends[layer, b, :, lanes] * after, axis=0, keepdims=True)
        x.outer[layer, b, :, lanes] = inner

    kept = (x.kept_heads, x.kept_scores, x.kept_reads, x.kept_writes)

    def grads(layer, b, tile, u, dy):
        w, r, lanes = x.w_all[layer, b], x.r_all[layer, b], tiles[tile]
        wide, wide_dy = u.astype(F32), dy.astype(F32)
        terms = wide_dy * x.outer[layer, b, :, lanes] - wide * x.inner[layer, b, :, lanes]
        through = jnp.where(iota((8, step), 0) == 7, x.through[layer, b, :, lanes], 0.0)
        terms, terms_low = two(rows_of(terms[: length - 8], terms[length - 8 :] + through))
        high = x.us[layer, b, 0, :, lanes]
        other = rows_of(x.turns[layer, b, 0, :, lanes], high[half:])
        dys = x.dys[layer, b, :, lanes]
        dy_a, dy_z = dys[:half], dys[half:]
        dscores = rows_of(nt(dy_a, high), nt(dy_z, other))
        if layer == 0:
            rest = x.us[layer, b, 1, :, lanes]
            other_low = rows_of(x.turns[layer, b, 1, :, lanes], rest[half:])
            dscores = dscores + rows_of(nt(dy_a, rest), nt(dy_z, other_low))
        totals = (
            nn(terms, picks[lanes]) + nn(terms_low, picks[lanes]),
            dscores,
            rows_of(nt(dy_a, x.starts_a[layer, b, :, lanes]), nt(dy_z, x.starts_z[layer, b, :, lanes])),
            rows_of(nt(high[:half], x.ends_a[layer, b, :, lanes]), nt(high[half:], x.ends_z[layer, b, :, lanes])),
        )
        totals = (totals[0], jnp.where(lower, totals[1], 0.0)) + totals[2:]
        if tile:
            totals = tuple(part + ref[layer, b] for part, ref in zip(totals, kept))
        if tile < len(tiles) - 1:
            for part, ref in zip(totals, kept):
                ref[layer, b] = part
            return
        by_head, by_head_low = two(totals[0])
        x.decays[layer, b] = tn(by_head, since) + tn(by_head_low, since)
        dscores, dscores_low = two(totals[1])
        x.params[layer, b, 0] = tn(dscores, r) + tn(dscores_low, r) + totals[3]
        x.params[layer, b, 1] = nn(dscores, w) + nn(dscores_low, w) + totals[2]

    decays_in = (x.decays1_in, x.decays2_in)

    def input_copy(to, tile, slot):
        at = pl.ds(pl.multiple_of(me * features + tiles[tile].start, step), step)
        return copy_to("seq", to, x.du1.at[to, :, tiles[tile]], x.dinput.at[:, at], x.input, tile, slot)

    def decay_copy(layer, to, slot):
        return copy_to("seq", to, x.decays.at[layer, to], decays_in[layer].at[me], x.decay, layer, slot)

    def twin_copy(layer, owner, slot):
        return copy_to("seq", twin, x.params.at[layer, owner], x.twins.at[layer, slot], x.twin, layer, slot)

    def leave(layer):
        for d in range(1, n):
            decay_copy(layer, lax.rem(me + d, n), d - 1).start()
        for away in range(chips):
            twin_copy(layer, device(away, 1), away).start()

    chip_copies = []

    def leave_chip(layer):
        for away in range(1, chips):
            owner = device(away, 0)
            twin_copy(layer, device(away, 1), away).wait_recv()
            total = x.params[layer, owner] + x.twins[layer, away]
            x.chip_sums[layer, away] = total.astype(BF16)
            copy = copy_to(
                "seq", owner, x.chip_sums.at[layer, away], x.chips_in.at[layer, away], x.chip, layer, away
            )
            copy.start()
            chip_copies.append(copy)

    hear(2)
    own_load.wait()
    x.skips[...] = jnp.zeros_like(x.skips)
    clip_copies = []

    def send_skips():
        channel, head = iota((features, length), 0) // size, iota((features, length), 1)
        x.by_head[...] = nn(x.skips[...], (channel == head).astype(F32), HIGHEST) * factor
        for d in range(1, clips):
            to = lax.rem(clip + d, clips)
            copy = copy_to("dp", to, x.by_head, x.clips_in.at[clip], x.clip, d - 1)
            copy.start()
            clip_copies.append(copy)
        x.clips_in[clip] = x.by_head[...]

    def pass_tile(tile):
        lanes, final = tiles[tile], tile == len(tiles) - 1

        wait_for(ct_at + 2 * tile)

        def back_second(i, carry):
            b = n - 1 - i
            x.du2[chunk(b), lanes] = back(1, b, lanes, x.ct_all[chunk(b), lanes])
            return carry

        lax.fori_loop(0, n, back_second, 0, unroll=4)

        def regrid_back(i, carry):
            x.dy1[chunk(i), lanes] = nn(x.take_first[i], x.du2[:, lanes]).astype(BF16)
            x.ct_first[chunk(i), lanes] = nn(x.take_first[i], x.ct_all[:, lanes]).astype(BF16)
            return carry

        lax.fori_loop(0, n, regrid_back, 0, unroll=4)
        adjoint[:, lanes] = jnp.zeros((adjoint.shape[0], step), F32)

        def back_first(i, carry):
            b = n - 1 - i
            x.du1[b, :, lanes] = back(0, b, lanes, x.dy1[chunk(b), lanes])
            return carry

        lax.fori_loop(0, n, back_first, 0, unroll=4)
        for d in range(1, n):
            input_copy(lax.rem(me + d, n), tile, d - 1).start()
        wait_for(u_at + 2 * tile)

        def first_layer(b, carry):
            def put(wide, value):
                x.y1[chunk(b), lanes] = value
                x.skips[0:1, lanes] += jnp.sum(wide * x.dy1[chunk(b), lanes].astype(F32), axis=0, keepdims=True)
                upstream = x.ct_first[chunk(b), lanes].astype(F32)
                x.skips[1:2, lanes] += jnp.sum(value.astype(F32) * upstream, axis=0, keepdims=True)

            forward(0, b, lanes, x.u_all[b, :, lanes], put)
            return carry

        lax.fori_loop(0, n, first_layer, 0, unroll=4)
        if final:
            hear(clips // 2 - 1)
            send_skips()

        def regrid(i, carry):
            x.u2[i, :, lanes] = nn(x.take_second[i], x.y1[:, lanes]).astype(BF16)
            return carry

        lax.fori_loop(0, n, regrid, 0, unroll=4)
        state[:, lanes] = jnp.zeros((state.shape[0], step), F32)

        def second_layer(b, carry):
            forward(1, b, lanes, x.u2[b, :, lanes], None)
            grads(0, b, tile, x.u_all[b, :, lanes], x.dy1[chunk(b), lanes])
            return carry

        lax.fori_loop(0, n, second_layer, 0, unroll=4)
        if final:
            leave(0)

        def second_grads(b, carry):
            grads(1, b, tile, x.u2[b, :, lanes], x.ct_all[chunk(b), lanes])
            return carry

        lax.fori_loop(0, n, second_grads, 0, unroll=4)
        if final:
            leave(1)
            leave_chip(0)
            leave_chip(1)

    for tile in range(len(tiles)):
        pass_tile(tile)
    for copy in clip_copies:
        copy.wait()
    x.summed[...] = jnp.sum(x.clips_in[...], axis=0)
    last = []
    for d in range(1, n):
        to = lax.rem(me + d, n)
        copy = copy_to("seq", to, x.summed, x.parts_in.at[me], x.part, d - 1)
        copy.start()
        last.append(copy)
    x.parts_in[me] = x.summed[...]
    own_input = pltpu.make_async_copy(x.du1.at[me], cut(x.dinput, me), x.load.at[0])
    own_input.start()
    for layer in range(2):
        decays_in[layer][me] = x.decays[layer, me]
    for layer, outs in enumerate(((x.dw1, x.dr1), (x.dw2, x.dr2))):
        twin_copy(layer, twin, 0).wait_recv()
        for k, out in enumerate(outs):
            total = x.params[layer, me, k] + x.twins[layer, 0, k]
            if k == 0:
                for copy in chip_copies[layer * (chips - 1) : (layer + 1) * (chips - 1)]:
                    copy.wait_recv()
            for away in range(1, chips):
                total = total + x.chips_in[layer, away, k].astype(F32)
            out[...] = total.astype(BF16)
    for group in arriving:
        for copy in group:
            copy.wait_send()
    for copy in far + near + chip_copies:
        copy.wait_send()
    for layer in range(2):
        for away in range(chips):
            twin_copy(layer, device(away, 1), away).wait_send()
    for d in range(1, n):
        to = lax.rem(me + d, n)
        last += [input_copy(to, tile, d - 1) for tile in range(len(tiles))]
        last += [decay_copy(0, to, d - 1), decay_copy(1, to, d - 1)]
    for copy in last:
        copy.wait()
    for s in range(n):
        for k, out in enumerate((x.dk1, x.dk2)):
            out[:, s * heads : (s + 1) * heads] = x.parts_in[s, k : k + 1, :heads]
    own_input.wait()


def whole(n, clips, size, factor, *args):
    length, width = args[0].shape
    heads = args[3].shape[1]
    count = args[1].shape[1]
    features, half, chips = heads * size, length // 2, n // 2
    vmem = pl.BlockSpec(memory_space=pltpu.VMEM)
    smem = pl.BlockSpec(memory_space=pltpu.SMEM)
    away = pl.BlockSpec(memory_space=pl.ANY)
    param, decay, gain = (length, count), (n, heads, length), (2, features)
    wide, flat, held, square = (n, length, features), (n * length, features), (n, count, features), (n, length, length)
    order, pick, pair = (n, 1, length), (n, length, n * length), (2, length, count)
    outs = (((length, width), BF16),) + ((param, BF16),) * 4 + ((decay, F32),) * 2 + (((1, n * heads), F32),) * 2
    scratch = dict(
        ct_out=((length, width), BF16),
        ct_wide=((length, width), F32),
        u_all=(wide, BF16),
        ct_all=(flat, BF16),
        ct_first=(flat, BF16),
        w_all=((2, n) + param, BF16),
        r_all=((2, n) + param, BF16),
        g_all=((2,) + decay, F32),
        o1_all=(order, jnp.int32),
        o2_all=(order, jnp.int32),
        grown=((2,) + wide, F32),
        shrunk=((2,) + wide, F32),
        sums=((2, n, 8, features), F32),
        fore=((2,) + square, BF16),
        fore_low=((2,) + square, BF16),
        back=((2,) + square, BF16),
        back_low=((2,) + square, BF16),
        take_first=(pick, BF16),
        take_second=(pick, BF16),
        du2=(flat, BF16),
        dy1=(flat, BF16),
        y1=(flat, BF16),
        u2=(wide, BF16),
        du1=(wide, BF16),
        dys=((2,) + wide, BF16),
        ends=((2,) + held, F32),
        ends_a=((2,) + held, BF16),
        ends_z=((2,) + held, BF16),
        inner=((2,) + wide, F32),
        outer=((2,) + wide, F32),
        us=((2, n, 2, length, features), BF16),
        turns=((2, n, 2, half, features), BF16),
        starts_a=((2,) + held, BF16),
        starts_z=((2,) + held, BF16),
        through=((2, n, 1, features), F32),
        kept_heads=((2, n, length, heads), F32),
        kept_scores=((2,) + square, F32),
        kept_reads=((2, n) + param, F32),
        kept_writes=((2, n) + param, F32),
        state=((count, features), F32),
        adjoint=((count, features), F32),
        params=((2, n) + pair, F32),
        twins=((2, chips) + pair, F32),
        chip_sums=((2, chips) + pair, BF16),
        chips_in=((2, chips) + pair, BF16),
        decays=((2,) + decay, F32),
        skips=(gain, F32),
        by_head=((2, length), F32),
        clips_in=((clips, 2, length), F32),
        summed=((2, length), F32),
        parts_in=((n, 2, length), F32),
    )
    sems = dict(
        move=(n - 1, 4 + 2 * max(1, features // (2 * length))),
        near=(n - 1, 4),
        input=(max(1, features // (2 * length)), n - 1),
        decay=(2, n - 1),
        twin=(2, chips),
        chip=(2, chips),
        clip=(clips - 1,),
        part=(n - 1,),
    )
    taken = sum(math.prod(shape) * jnp.dtype(kind).itemsize for shape, kind in scratch.values())
    return pl.pallas_call(
        functools.partial(whole_kernel, n, clips, size, factor, tuple(scratch), tuple(sems)),
        out_shape=tuple(jax.ShapeDtypeStruct(*out) for out in outs),
        in_specs=[away] + [vmem] * 3 + [smem] + [vmem] * 3 + [smem] + [vmem] * 2 + [away],
        out_specs=[away] + [vmem] * 8,
        scratch_shapes=[pltpu.VMEM(*one) for one in scratch.values()]
        + [pltpu.SemaphoreType.DMA(shape) for shape in sems.values() for _ in range(2)]
        + [pltpu.SemaphoreType.DMA((2,)), pltpu.SemaphoreType.REGULAR((clips // 2 - 1,))],
        compiler_params=pltpu.CompilerParams(
            collective_id=0, has_side_effects=True
        ),
        name="whole",
    )(*args)


def gather_kernel(count, *refs):
    sources, results, held, sems = refs[:count], refs[count : 2 * count], refs[2 * count : 3 * count], refs[-2:]
    pieces = []
    for k, source in enumerate(sources):
        step = max(source.shape[0] // 4, 1) if k == 0 else source.shape[0]
        pieces += [(k, pl.ds(at, step)) for at in range(0, source.shape[0], step)]
    loads, stores = [], []
    for at, (k, rows) in enumerate(pieces):
        loads.append(pltpu.make_async_copy(sources[k].at[rows], held[k].at[rows], sems[0].at[at]))
        stores.append(pltpu.make_async_copy(held[k].at[rows], results[k].at[rows], sems[1].at[at]))
        loads[-1].start()
    for load, store in zip(loads, stores):
        load.wait()
        store.start()
    for store in stores:
        store.wait()


def gather(*results):
    away = pl.BlockSpec(memory_space=pl.ANY)
    count = len(results)
    return pl.pallas_call(
        functools.partial(gather_kernel, count),
        out_shape=tuple(jax.ShapeDtypeStruct(one.shape, one.dtype) for one in results),
        in_specs=[away] * count,
        out_specs=[away] * count,
        scratch_shapes=[pltpu.VMEM(one.shape, one.dtype) for one in results]
        + [pltpu.SemaphoreType.DMA((count + 3,))] * 2,
        name="gather",
    )(*results)


def on_device(n, clips, u, w1, r1, g1, k1, w2, r2, g2, k2, o1, o2, ct):
    length, features = u.shape[1:]
    head_count = k1.shape[0]
    size = features // head_count
    heads = head_count // n

    def by_device(g):
        return g.reshape(n, heads, length)

    results = whole(
        n,
        clips,
        size,
        1.0 / math.sqrt(clips * n * length * size),
        u[0],
        w1[0],
        r1[0],
        by_device(g1),
        k1,
        w2[0],
        r2[0],
        by_device(g2),
        k2,
        o1[None],
        o2[None],
        ct[0],
    )
    du, dw1, dr1, dw2, dr2, dg1, dg2, dk1, dk2 = gather(*results)
    return (
        du[None],
        dw1[None],
        dr1[None],
        dg1.reshape(1, head_count, length),
        dk1[0],
        dw2[None],
        dr2[None],
        dg2.reshape(1, head_count, length),
        dk2[0],
    )


def solution(mesh):
    tokens, decay = P("dp", "seq", None), P("dp", None, "seq")
    return jax.shard_map(
        functools.partial(on_device, mesh.shape["seq"], mesh.shape["dp"]),
        mesh=mesh,
        in_specs=(tokens, tokens, tokens, decay, P(), tokens, tokens, decay, P(), P("seq"), P("seq"), tokens),
        out_specs=(tokens, tokens, tokens, decay, P(), tokens, tokens, decay, P()),
        check_vma=False,
    )
```

time: 36.5 us -> 35.4 us (0.970)
  Pallas kernels: 35.6 us -> 34.5 us
    pallas_call x2, Pallas kernels: 35.6 us -> 34.5 us  [the longest x1 32.5 us: whole(): pl.pallas_call(functools.partial(whole_kernel, n, clips, size, factor, tu...]
where the time goes in v3:
time: 35.4 us; the launch traced here: 35.2 us
  Pallas kernels  34.5 us (97%)
  between operations  0.65 us (2%)
    pallas_call x1, Pallas kernels, whole(): pl.pallas_call(functools.partial(whole_kernel, n, clips, size, factor, tu...  32.5 us
    pallas_call x1, Pallas kernels, gather(): pl.pallas_call(functools.partial(gather_kernel, count), out_shape=tuple((...  2.01 us

profile of v3, /device:TPU:0, one launch (start us, length us, event | category | flops | bytes accessed | tf_op | source)
XLA Modules:
  0.0 35.2 jit_solution(15462759416925750189)
XLA Ops:
  0.6 32.5 %whole.1 = (bf16[128,2048]{1,0:T(8,128)(2,1)}, bf16[128,128]{1,0:T(8,128)(2,1)}, bf16[128,128]{1,0:T(8,128)(2,1)}, bf16[128,128]{1,0:T(8,128)(2,1)}, bf16[128,12...) custom-call(bf16[128,2048]{1,0:T(8,128)(2,1)} %bitcast.20, ...), custom_call_target="tpu_custom_call" | custom-call | tf_op jit(solution)/shard_map/whole/pallas_call | solution.py:612
  33.2 2.0 %gather.1 = (bf16[128,2048]{1,0:T(8,128)(2,1)}, bf16[128,128]{1,0:T(8,128)(2,1)}, bf16[128,128]{1,0:T(8,128)(2,1)}, bf16[128,128]{1,0:T(8,128)(2,1)}, bf16[128,1...) custom-call(bf16[128,2048]{1,0:T(8,128)(2,1)} %get-tuple-element.27.refs, ...), custom_call_target="tpu_custom_call" | custom-call | tf_op jit(solution)/shard_map/gather/pallas_call | solution.py:648

commit v4 on v3

--- a/solution.py
+++ b/solution.py
@@ -381,11 +381,13 @@
     def twin_copy(layer, owner, slot):
         return copy_to("seq", twin, x.params.at[layer, owner], x.twins.at[layer, slot], x.twin, layer, slot)
 
-    def leave(layer):
+    def leave(layer, ways):
+        for away in ways:
+            twin_copy(layer, device(away, 1), away).start()
+
+    def leave_decays(layer):
         for d in range(1, n):
             decay_copy(layer, lax.rem(me + d, n), d - 1).start()
-        for away in range(chips):
-            twin_copy(layer, device(away, 1), away).start()
 
     chip_copies = []
 
@@ -475,17 +477,23 @@
 
         lax.fori_loop(0, n, second_layer, 0, unroll=4)
         if final:
-            leave(0)
-
-        def second_grads(b, carry):
+            leave(0, range(chips))
+            leave_decays(0)
+
+        def second_grads(i, carry):
+            b = lax.rem(2 * chip + 2 + i, n)
             grads(1, b, tile, x.u2[b, :, lanes], x.ct_all[chunk(b), lanes])
             return carry
 
-        lax.fori_loop(0, n, second_grads, 0, unroll=4)
+        lax.fori_loop(0, n - 2, second_grads, 0, unroll=2)
         if final:
-            leave(1)
+            leave(1, range(1, chips))
             leave_chip(0)
+        lax.fori_loop(n - 2, n, second_grads, 0, unroll=2)
+        if final:
             leave_chip(1)
+            leave(1, range(1))
+            leave_decays(1)
 
     for tile in range(len(tiles)):
         pass_tile(tile)

time: 35.4 us -> 35.1 us (level)
    pallas_call x1, Pallas kernels: 32.5 us -> 32.2 us  [whole(): pl.pallas_call(functools.partial(whole_kernel, n, clips, size, factor, tu...]
where the time goes in v4:
time: 35.1 us; the launch traced here: 34.8 us
  Pallas kernels  34.2 us (97%)
  between operations  0.65 us (2%)
    pallas_call x1, Pallas kernels, whole(): pl.pallas_call(functools.partial(whole_kernel, n, clips, size, factor, tu...  32.2 us
    pallas_call x1, Pallas kernels, gather(): pl.pallas_call(functools.partial(gather_kernel, count), out_shape=tuple((...  2.01 us

profile of v4, /device:TPU:0, one launch (start us, length us, event | category | flops | bytes accessed | tf_op | source)
XLA Modules:
  0.0 34.8 jit_solution(9676686592841738445)
XLA Ops:
  0.6 32.2 %whole.1 = (bf16[128,2048]{1,0:T(8,128)(2,1)}, bf16[128,128]{1,0:T(8,128)(2,1)}, bf16[128,128]{1,0:T(8,128)(2,1)}, bf16[128,128]{1,0:T(8,128)(2,1)}, bf16[128,12...) custom-call(bf16[128,2048]{1,0:T(8,128)(2,1)} %bitcast.20, ...), custom_call_target="tpu_custom_call" | custom-call | tf_op jit(solution)/shard_map/whole/pallas_call | solution.py:620
  32.8 2.0 %gather.1 = (bf16[128,2048]{1,0:T(8,128)(2,1)}, bf16[128,128]{1,0:T(8,128)(2,1)}, bf16[128,128]{1,0:T(8,128)(2,1)}, bf16[128,128]{1,0:T(8,128)(2,1)}, bf16[128,1...) custom-call(bf16[128,2048]{1,0:T(8,128)(2,1)} %get-tuple-element.27.refs, ...), custom_call_target="tpu_custom_call" | custom-call | tf_op jit(solution)/shard_map/gather/pallas_call | solution.py:656

commit v5 on v4

--- a/solution.py
+++ b/solution.py
@@ -410,7 +410,9 @@
 
     def send_skips():
         channel, head = iota((features, length), 0) // size, iota((features, length), 1)
-        x.by_head[...] = nn(x.skips[...], (channel == head).astype(F32), HIGHEST) * factor
+        by_channel, chosen = x.skips[...], (channel == head).astype(BF16)
+        high, rest = two(by_channel)
+        x.by_head[...] = (nn(high, chosen) + nn(rest, chosen)) * factor
         for d in range(1, clips):
             to = lax.rem(clip + d, clips)
             copy = copy_to("dp", to, x.by_head, x.clips_in.at[clip], x.clip, d - 1)

time: 35.1 us -> 35 us (level)
  no operation moved by 1% of the time
where the time goes in v5:
time: 35 us; the launch traced here: 34.7 us
  Pallas kernels  34.1 us (97%)
  between operations  0.65 us (2%)
    pallas_call x1, Pallas kernels, whole(): pl.pallas_call(functools.partial(whole_kernel, n, clips, size, factor, tu...  32.1 us
    pallas_call x1, Pallas kernels, gather(): pl.pallas_call(functools.partial(gather_kernel, count), out_shape=tuple((...  2.01 us

profile of v5, /device:TPU:0, one launch (start us, length us, event | category | flops | bytes accessed | tf_op | source)
XLA Modules:
  0.0 34.7 jit_solution(992804000682680864)
XLA Ops:
  0.6 32.1 %whole.1 = (bf16[128,2048]{1,0:T(8,128)(2,1)}, bf16[128,128]{1,0:T(8,128)(2,1)}, bf16[128,128]{1,0:T(8,128)(2,1)}, bf16[128,128]{1,0:T(8,128)(2,1)}, bf16[128,12...) custom-call(bf16[128,2048]{1,0:T(8,128)(2,1)} %bitcast.20, ...), custom_call_target="tpu_custom_call" | custom-call | tf_op jit(solution)/shard_map/whole/pallas_call | solution.py:622
  32.7 2.0 %gather.1 = (bf16[128,2048]{1,0:T(8,128)(2,1)}, bf16[128,128]{1,0:T(8,128)(2,1)}, bf16[128,128]{1,0:T(8,128)(2,1)}, bf16[128,128]{1,0:T(8,128)(2,1)}, bf16[128,1...) custom-call(bf16[128,2048]{1,0:T(8,128)(2,1)} %get-tuple-element.27.refs, ...), custom_call_target="tpu_custom_call" | custom-call | tf_op jit(solution)/shard_map/gather/pallas_call | solution.py:658
